TPU v7x, 32 devices: a whole 2x2x4 slice. The times are simulated.
32 devices in a mesh: lat: 4 (over x, core), lon: 8 (over z, y).
Axes of the slice: x: 2, y: 2, z: 4, core: 2. Of those that a mesh axis runs over, the one named last changes fastest.
Arguments:
- tokens: bfloat16 [4, 56, 32, 1536], P(None, 'lat', 'lon'), may hold values from -400 to 400, as said below
- in_bounds: int32 [5], replicated, may hold values from 0 to 47, as said below
- out_bounds: int32 [5], replicated, may hold values from 0 to 24, as said below
- down_gain: float32 [768], replicated, may hold values from 0.25 to 1.75
- down_bias: float32 [768], replicated, may hold values from -1 to 1
- down_weight: bfloat16 [768, 384], replicated, may hold values from -0.21875 to 0.21875
- up_weight: bfloat16 [384, 768], replicated, may hold values from -0.3125 to 0.3125
- up_gain: float32 [192], replicated, may hold values from 0.25 to 1.75
- up_bias: float32 [192], replicated, may hold values from -1 to 1
- out_weight: bfloat16 [192, 192], replicated, may hold values from -0.4375 to 0.4375
Outputs:
- merged: bfloat16 [4, 32, 16, 3072], P(None, 'lat', 'lon')
- upsampled: bfloat16 [4, 56, 32, 1536], P(None, 'lat', 'lon')
Inputs may be any that keep to these rules, and one draw needn't show every extreme that they name: `tokens`: band b's fine rows stand in its slots from the first one on; slots past the band's count hold values that no output reads. in_bounds[0] = 0, in_bounds[4] = 47; each band has 10 to 14 fine rows, and some band has 14. out_bounds[0] = 0, out_bounds[4] = 24; each band has 4 to 8 merged rows, and some band has 8. For 0 < b < 4, 2 * out_bounds[b] - in_bounds[b] is 1 to 3, and 3 for some b; so merged band b covers fine rows from band b's first on to at most 3 rows past its last (fine row 47 counting as zeros), and band b's fine rows need merged rows from at most 2 rows before merged band b's first up to its last, 2 being reached.
All inputs are finite; a program needn't handle non-finite values.
Results may differ from a plain program's by a relative error of at most 0.0069.
Values may be sent and summed in bfloat16 or wider, within the bound.
A program may use at most 64 MiB of HBM per device.

v0:
```python
import functools

import jax
import jax.numpy as jnp
from jax import lax
from jax.experimental import pallas as pl
from jax.experimental.pallas import tpu as pltpu
from jax.sharding import PartitionSpec as P

HALO = 3
LANES_OF_LEVELS = 4
TILE = 128
MESH = pl.DeviceIdType.MESH


def norm(values, scale_vec, shift_vec):
    center = jnp.mean(values, axis=-1, keepdims=True)
    off = values - center
    spread = jnp.mean(off * off, axis=-1, keepdims=True)
    return off * lax.rsqrt(spread + 1e-05) * scale_vec + shift_vec


def kernel(
    n_lat,
    n_lon,
    in_b,
    out_b,
    t_ref,
    dw_hbm,
    uw_hbm,
    ow_hbm,
    dg_ref,
    db_ref,
    ug_ref,
    ub_ref,
    mo_ref,
    fo_ref,
    comb,
    west_in,
    east_in,
    top_in,
    bot_in,
    top_w,
    top_e,
    bot_w,
    bot_e,
    tail,
    tail_w,
    tail_e,
    nrm,
    turn_in,
    turn_merged,
    turn_fine,
    dw,
    uw,
    ow,
    local_sem,
    send_sem,
    recv_sem,
):
    members, slots, cols, packed = t_ref.shape
    merged_slots = mo_ref.shape[1]
    _, _, sub, lanes = comb.shape
    halves = sub // members
    chan = lanes // LANES_OF_LEVELS
    tiles = lanes // TILE
    total = slots + 2 * HALO
    rows = 2 * merged_slots + 4
    mid_lo, mid_hi = HALO, slots // 2
    lat = lax.axis_index("lat")
    lon = lax.axis_index("lon")
    east = {"lat": lat, "lon": lax.rem(lon + 1, n_lon)}
    west = {"lat": lat, "lon": lax.rem(lon + n_lon - 1, n_lon)}
    above = {"lat": jnp.maximum(lat - 1, 0), "lon": lon}
    below = {"lat": jnp.minimum(lat + 1, n_lat - 1), "lon": lon}
    has_above = lat > 0
    has_below = lat < n_lat - 1

    loads = [
        pltpu.make_async_copy(dw_hbm, dw, local_sem.at[0]),
        pltpu.make_async_copy(uw_hbm, uw, local_sem.at[1]),
        pltpu.make_async_copy(ow_hbm, ow, local_sem.at[2]),
    ]
    for load in loads:
        load.start()

    barrier = pltpu.get_barrier_semaphore()
    pl.semaphore_signal(barrier, inc=1, device_id=east, device_id_type=MESH)
    pl.semaphore_signal(barrier, inc=1, device_id=west, device_id_type=MESH)

    @pl.when(has_above)
    def _():
        pl.semaphore_signal(barrier, inc=1, device_id=above, device_id_type=MESH)

    @pl.when(has_below)
    def _():
        pl.semaphore_signal(barrier, inc=1, device_id=below, device_id_type=MESH)

    for r in range(slots):
        for member in range(members):
            row = t_ref[member, r].astype(jnp.float32)
            for half in range(halves):
                at = (half * members + member) * cols
                for t in range(tiles):
                    lane = half * lanes + t * TILE
                    turn_in[r, t, at : at + cols, :] = row[:, lane : lane + TILE]

    def take_column(x):
        for r in range(slots):
            for t in range(tiles):
                comb[1 + x, HALO + r, :, t * TILE : (t + 1) * TILE] = turn_in[
                    r, t, pl.ds(x, sub, stride=cols), :
                ].astype(jnp.bfloat16)

    take_column(cols - 1)
    take_column(0)

    pl.semaphore_wait(barrier, 2 + has_above.astype(jnp.int32) + has_below.astype(jnp.int32))

    def remote(src, dst, slot, device):
        return pltpu.make_async_remote_copy(
            src_ref=src,
            dst_ref=dst,
            send_sem=send_sem.at[slot],
            recv_sem=recv_sem.at[slot],
            device_id=device,
            device_id_type=MESH,
        )

    spans = [(0, mid_lo), (mid_hi, slots), (mid_lo, mid_hi)]
    to_east, to_west = [], []
    for i, (lo, hi) in enumerate(spans):
        span = pl.ds(lo, hi - lo)
        held = pl.ds(HALO + lo, hi - lo)
        to_east.append(remote(comb.at[cols, held], west_in.at[span], i, east))
        to_west.append(remote(comb.at[1, held], east_in.at[span], 3 + i, west))
    up = remote(comb.at[pl.ds(1, cols), pl.ds(HALO, HALO)], bot_in, 6, above)
    down = remote(tail, top_in, 7, below)
    head = pl.ds(0, HALO)
    up_w = remote(west_in.at[head], bot_w, 8, above)
    up_e = remote(east_in.at[head], bot_e, 9, above)
    down_w = remote(tail_w, top_w, 10, below)
    down_e = remote(tail_e, top_e, 11, below)

    for i in range(3):
        to_east[i].start()
        to_west[i].start()

    for x in range(1, cols - 1):
        take_column(x)

    @pl.when(has_above)
    def _():
        up.start()

    start_in = in_b[lat]
    end_in = in_b[lat + 1]
    count = end_in - start_in
    shift = 2 * out_b[lat] - start_in
    past = count - shift + 4

    for x in range(cols):
        for i in range(HALO):
            tail[x, i] = comb[1 + x, count + i]

    @pl.when(has_below)
    def _():
        down.start()

    for load in loads:
        load.wait()

    def place(r):
        inside = jnp.maximum(r + shift - 1, 0)
        outside = jnp.minimum(HALO + slots + r - past, total - 1)
        return jnp.where(r < past, inside, outside)

    spots = [place(r) for r in range(rows)]

    dg = dg_ref[...][None]
    db = db_ref[...][None]
    ug = ug_ref[...][None]
    ub = ub_ref[...][None]

    def compute(j, ms):
        nm = len(ms)
        size = LANES_OF_LEVELS * nm * sub
        for k in range(0, nm, 2):
            blocks = []
            for c in range(2):
                for a in range(2):
                    blocks.append(
                        jnp.concatenate(
                            [comb[2 * j + c, spots[2 * m + a]].astype(jnp.float32) for m in ms[k : k + 2]],
                            axis=0,
                        )
                    )
            for level in range(LANES_OF_LEVELS):
                cut = slice(level * chan, (level + 1) * chan)
                pieces = jnp.concatenate([block[:, cut] for block in blocks], axis=1)
                at = (level * nm + k) * sub
                nrm[at : at + 2 * sub, :] = norm(pieces, dg, db).astype(jnp.bfloat16)
        wide = jnp.dot(nrm[0:size, :], dw[...], preferred_element_type=jnp.float32)
        coarse = wide.astype(jnp.bfloat16)
        if j < 2:
            for i, m in enumerate(ms):
                if m < 2:
                    continue
                for level in range(LANES_OF_LEVELS):
                    at = (level * nm + i) * sub
                    for t in range(2 * chan // TILE):
                        turn_merged[
                            m - 2, level * 2 * chan // TILE + t, pl.ds(j, sub, stride=cols // 2), :
                        ] = wide[at : at + sub, t * TILE : (t + 1) * TILE]
        for c, x in (((1, 0),), ((0, 1), (1, 2)), ((0, 3),))[j]:
            spread = jnp.dot(
                coarse, uw[:, c * 2 * chan : (c + 1) * 2 * chan], preferred_element_type=jnp.float32
            ).astype(jnp.bfloat16)
            spread = spread.astype(jnp.float32)
            for a in range(2):
                half = norm(spread[:, a * chan : (a + 1) * chan], ug, ub).astype(jnp.bfloat16)
                done = jnp.dot(half, ow[...], preferred_element_type=jnp.float32)
                for i, m in enumerate(ms):
                    line = jnp.concatenate(
                        [
                            done[(level * nm + i) * sub : (level * nm + i + 1) * sub]
                            for level in range(LANES_OF_LEVELS)
                        ],
                        axis=1,
                    )
                    for t in range(tiles):
                        turn_fine[2 * m + a, t, pl.ds(x, sub, stride=cols), :] = line[
                            :, t * TILE : (t + 1) * TILE
                        ]

    own = pl.ds(1, cols)

    @pl.when(has_above)
    def _():
        down.wait_recv()

    @pl.when(has_below)
    def _():
        up.wait_recv()
        comb[own, HALO + slots : total] = bot_in[...]

    @pl.when(jnp.logical_not(has_below))
    def _():
        comb[:, HALO + slots : total] = jnp.zeros((cols + 2, HALO, sub, lanes), jnp.bfloat16)

    @pl.when(has_above)
    def _():
        comb[own, 0:HALO] = top_in[...]

    @pl.when(jnp.logical_not(has_above))
    def _():
        comb[:, 0:HALO] = jnp.zeros((cols + 2, HALO, sub, lanes), jnp.bfloat16)

    merged_rows = rows // 2
    compute(1, list(range(merged_rows)))

    for i in range(2):
        lo, hi = spans[i]
        to_east[i].wait_recv()
        comb[0, HALO + lo : HALO + hi] = west_in[lo:hi]
        to_west[i].wait_recv()
        comb[cols + 1, HALO + lo : HALO + hi] = east_in[lo:hi]
    for i in range(HALO):
        tail_w[i] = comb[0, count + i]
        tail_e[i] = comb[cols + 1, count + i]

    @pl.when(has_above)
    def _():
        up_w.start()
        up_e.start()

    @pl.when(has_below)
    def _():
        down_w.start()
        down_e.start()

    lo, hi = spans[2]
    to_east[2].wait_recv()
    comb[0, HALO + lo : HALO + hi] = west_in[lo:hi]
    to_west[2].wait_recv()
    comb[cols + 1, HALO + lo : HALO + hi] = east_in[lo:hi]

    @pl.when(has_above)
    def _():
        down_w.wait_recv()
        comb[0, 0:HALO] = top_w[...]
        down_e.wait_recv()
        comb[cols + 1, 0:HALO] = top_e[...]

    @pl.when(has_below)
    def _():
        up_w.wait_recv()
        comb[0, HALO + slots : total] = bot_w[...]
        up_e.wait_recv()
        comb[cols + 1, HALO + slots : total] = bot_e[...]

    def put_out(value, live, slot, out_ref, width, span):
        value = jnp.where(live, value, 0.0).astype(jnp.bfloat16)
        for half in range(halves):
            for member in range(members):
                at = (half * members + member) * width
                out_ref[member, slot, :, half * span : (half + 1) * span] = jnp.concatenate(
                    [value[t, at : at + width] for t in range(span // TILE)], axis=1
                )

    compute(0, list(range(merged_rows)))
    count_out = out_b[lat + 1] - out_b[lat]
    for m in range(merged_slots):
        put_out(turn_merged[m], m < count_out, m, mo_ref, cols // 2, 2 * lanes)
    compute(2, list(range(merged_rows)))
    for k in range(slots):
        put_out(turn_fine[4 - shift + k], k < count, k, fo_ref, cols, lanes)

    for copy in to_east + to_west:
        copy.wait_send()

    @pl.when(has_above)
    def _():
        up.wait_send()
        up_w.wait_send()
        up_e.wait_send()

    @pl.when(has_below)
    def _():
        down.wait_send()
        down_w.wait_send()
        down_e.wait_send()


def body(
    tokens,
    in_bounds,
    out_bounds,
    down_gain,
    down_bias,
    down_weight,
    up_weight,
    up_gain,
    up_bias,
    out_weight,
):
    members, slots, cols, packed = tokens.shape
    chan = down_weight.shape[0] // 4
    halves = packed // (chan * LANES_OF_LEVELS)
    lanes = chan * LANES_OF_LEVELS
    sub = halves * members
    merged_slots = slots // 2 + 1
    half_cols = cols // 2
    rows = 2 * merged_slots + 4
    total = slots + 2 * HALO
    bf16 = jnp.bfloat16
    n_lat = lax.axis_size("lat")
    n_lon = lax.axis_size("lon")
    smem = pl.BlockSpec(memory_space=pltpu.SMEM)
    vmem = pl.BlockSpec(memory_space=pltpu.VMEM)
    hbm = pl.BlockSpec(memory_space=pl.ANY)
    column = pltpu.VMEM((slots, sub, lanes), bf16)
    patch = pltpu.VMEM((cols, HALO, sub, lanes), bf16)
    corner = pltpu.VMEM((HALO, sub, lanes), bf16)
    return pl.pallas_call(
        functools.partial(kernel, n_lat, n_lon),
        out_shape=(
            jax.ShapeDtypeStruct((members, merged_slots, half_cols, 2 * packed), bf16),
            jax.ShapeDtypeStruct(tokens.shape, bf16),
        ),
        in_specs=[smem, smem, vmem, hbm, hbm, hbm, vmem, vmem, vmem, vmem],
        out_specs=(vmem, vmem),
        scratch_shapes=[
            pltpu.VMEM((cols + 2, total, sub, lanes), bf16),
            column,
            column,
            patch,
            patch,
            corner,
            corner,
            corner,
            corner,
            patch,
            corner,
            corner,
            pltpu.VMEM((LANES_OF_LEVELS * rows // 2 * sub, 4 * chan), bf16),
            pltpu.VMEM((slots, lanes // TILE, sub * cols, TILE), jnp.float32),
            pltpu.VMEM((merged_slots, 2 * lanes // TILE, sub * half_cols, TILE), jnp.float32),
            pltpu.VMEM((rows, lanes // TILE, sub * cols, TILE), jnp.float32),
            pltpu.VMEM(down_weight.shape, bf16),
            pltpu.VMEM(up_weight.shape, bf16),
            pltpu.VMEM(out_weight.shape, bf16),
            pltpu.SemaphoreType.DMA((3,)),
            pltpu.SemaphoreType.DMA((12,)),
            pltpu.SemaphoreType.DMA((12,)),
        ],
        compiler_params=pltpu.CompilerParams(collective_id=0, has_side_effects=True),
    )(
        in_bounds,
        out_bounds,
        tokens,
        down_weight,
        up_weight,
        out_weight,
        down_gain,
        down_bias,
        up_gain,
        up_bias,
    )


def solution(mesh):
    return jax.shard_map(
        body,
        mesh=mesh,
        in_specs=(P(None, "lat", "lon", None), P(), P(), P(), P(), P(), P(), P(), P(), P()),
        out_specs=(P(None, "lat", "lon", None), P(None, "lat", "lon", None)),
        check_vma=False,
    )
```

profile of v0, /device:TPU:0, one launch (start us, length us, event | category | flops | bytes accessed | tf_op | source)
XLA Modules:
  0.0 27.1 jit_solution(3620627070311629431)
XLA Ops:
  0.6 23.5 %shard_map.113 = (bf16[4,8,2,3072]{3,2,1,0:T(2,128)(2,1)}, bf16[4,14,4,1536]{3,2,1,0:T(4,128)(2,1)}) custom-call(s32[5]{0:T(128)} %in_b.1, s32[5]{0:T(128)} %out_b.1, bf16[4,14,4,1536]{3,2,1,0:T(4,128)(2,1)} %t_ref.1, bf16[768,384]{1,0:T(8,128)(2,1)} %dw_hbm.1, bf16[384,768]{1,0:T(8,128)(2,1)} %uw_hbm.1, bf16[192,192]{1,0:T(8,128)(2,1)} %ow_hbm.1, ...), custom_call_target="tpu_custom_call" | custom-call | tf_op jit(solution)/shard_map/pallas_call | solution.py:365
  24.2 0.0 copy-start
  24.2 2.1 %copy.14 = bf16[4,8,2,3072]{3,2,1,0:T(2,128)(2,1)} copy(bf16[4,8,2,3072]{3,2,1,0:T(2,128)(2,1)} %get-tuple-element.4) | data formatting | bytes 786432
  26.3 0.0 copy-done
  26.3 0.8 %copy.15 = bf16[4,14,4,1536]{3,2,1,0:T(4,128)(2,1)} copy(bf16[4,14,4,1536]{3,2,1,0:T(4,128)(2,1)S(1)} %copy-done) | data formatting | bytes 1376256
Async XLA Ops:
  24.2 2.1 %copy-start = (bf16[4,14,4,1536]{3,2,1,0:T(4,128)(2,1)S(1)}, bf16[4,14,4,1536]{3,2,1,0:T(4,128)(2,1)}, u32[]{:S(2)}) copy-start(bf16[4,14,4,1536]{3,2,1,0:T(4,128)(2,1)} %get-tuple-element.5) | copy-start | bytes 2064388
where the time goes:
time: 27.5 us; the launch traced here: 27.1 us
  Pallas kernels  23.5 us (85%)
  local copies, waits for them, and re-layouts  2.93 us (11%)
  between operations  0.65 us (2%)
    pallas_call x1, Pallas kernels, body(): pl.pallas_call(functools.partial(kernel, n_lat, n_lon), out_shape=(jax.Sh...  23.5 us
    unnamed x4, local copies, waits for them, and re-layouts  2.93 us

commit v1 on v0

v1 whole, which is shorter than its diff:
```python
import functools

import jax
import jax.numpy as jnp
from jax import lax
from jax.experimental import pallas as pl
from jax.experimental.pallas import tpu as pltpu
from jax.sharding import PartitionSpec as P

HALO = 3
LANES_OF_LEVELS = 4
TILE = 128
MESH = pl.DeviceIdType.MESH


def pair_norm(blocks, size):
    low = lax.broadcasted_iota(jnp.int32, blocks[0][0].shape, 1) < TILE // 2
    inv = 1.0 / size

    def totals(tiles):
        one, mid, two = [functools.reduce(jnp.add, group) for group in zip(*tiles)]
        first = jnp.sum(one + jnp.where(low, mid, 0.0), axis=1, keepdims=True) * inv
        second = jnp.sum(two + jnp.where(low, 0.0, mid), axis=1, keepdims=True) * inv
        return first, second

    first, second = totals(blocks)
    mid = jnp.where(low, first, second)
    off = [(one - first, both - mid, two - second) for one, both, two in blocks]
    first, second = totals([tuple(v * v for v in tiles) for tiles in off])
    first, second = lax.rsqrt(first + 1e-05), lax.rsqrt(second + 1e-05)
    mid = jnp.where(low, first, second)
    return low, [(one * first, both * mid, two * second) for one, both, two in off]


def down_pieces(chan):
    half = chan - TILE
    even = [(0, b * chan, TILE) for b in range(4)] + [(0, b * chan + TILE, half) for b in range(4)]
    odd = [(1, b * chan + half, TILE) for b in range(4)] + [(1, b * chan, half) for b in (1, 0, 3, 2)]
    return even + odd


def thirds(value):
    return tuple(value[:, t * TILE : (t + 1) * TILE] for t in range(3))


def kernel(
    n_lat,
    n_lon,
    in_b_hbm,
    out_b_hbm,
    t_hbm,
    dw_hbm,
    uw_hbm,
    ow_hbm,
    dg_hbm,
    db_hbm,
    ug_hbm,
    ub_hbm,
    mo_ref,
    fo_ref,
    comb,
    west_in,
    east_in,
    top_in,
    bot_in,
    top_w,
    top_e,
    bot_w,
    bot_e,
    tail,
    tail_w,
    tail_e,
    nrm,
    coarse,
    renorm,
    turn_in,
    turn_merged,
    turn_fine,
    dw,
    uw,
    ow,
    ow_pad,
    down_vec,
    up_vec,
    t_ref,
    in_b,
    out_b,
    dg_ref,
    db_ref,
    ug_ref,
    ub_ref,
    local_sem,
    send_sem,
    recv_sem,
    wrap_sem,
):
    members, slots, cols, packed = t_ref.shape
    merged_slots = mo_ref.shape[1]
    _, _, sub, lanes = comb.shape
    halves = sub // members
    tiles = lanes // TILE
    total = slots + 2 * HALO
    rows = 2 * merged_slots + 4
    mid_lo, mid_hi = HALO, slots // 2
    lat = lax.axis_index("lat")
    lon = lax.axis_index("lon")
    east = {"lat": lat, "lon": lax.rem(lon + 1, n_lon)}
    west = {"lat": lat, "lon": lax.rem(lon + n_lon - 1, n_lon)}
    above = {"lat": jnp.maximum(lat - 1, 0), "lon": lon}
    below = {"lat": jnp.minimum(lat + 1, n_lat - 1), "lon": lon}
    has_above = lat > 0
    has_below = lat < n_lat - 1

    first = lon == 0
    last = lon == n_lon - 1
    barrier = pltpu.get_barrier_semaphore()
    pl.semaphore_signal(barrier, inc=1, device_id=west, device_id_type=MESH)

    @pl.when(jnp.logical_not(last))
    def _():
        pl.semaphore_signal(barrier, inc=1, device_id=east, device_id_type=MESH)

    @pl.when(has_above)
    def _():
        pl.semaphore_signal(barrier, inc=1, device_id=above, device_id_type=MESH)

    @pl.when(has_below)
    def _():
        pl.semaphore_signal(barrier, inc=1, device_id=below, device_id_type=MESH)

    pairs = [
        (t_hbm, t_ref),
        (in_b_hbm, in_b),
        (out_b_hbm, out_b),
        (uw_hbm, uw),
        (ow_hbm, ow),
        (dg_hbm, dg_ref),
        (db_hbm, db_ref),
        (ug_hbm, ug_ref),
        (ub_hbm, ub_ref),
    ]
    chan = lanes // LANES_OF_LEVELS
    short = chan - TILE
    for pos, (e, start, size) in enumerate(down_pieces(chan)):
        at = sum(piece[2] for piece in down_pieces(chan)[:pos] if piece[0] == e)
        pairs.append((dw_hbm.at[pl.ds(start, size)], dw.at[e, pl.ds(at, size)]))
    loads = [pltpu.make_async_copy(src, dst, local_sem.at[i]) for i, (src, dst) in enumerate(pairs)]
    for load in loads:
        load.start()
    loads[0].wait()

    for r in range(slots):
        for member in range(members):
            row = t_ref[member, r].astype(jnp.float32)
            for half in range(halves):
                at = (half * members + member) * cols
                for t in range(tiles):
                    lane = half * lanes + t * TILE
                    turn_in[r, t, at : at + cols, :] = row[:, lane : lane + TILE]

    def take_column(x):
        for r in range(slots):
            for t in range(tiles):
                comb[1 + x, HALO + r, :, t * TILE : (t + 1) * TILE] = turn_in[
                    r, t, pl.ds(x, sub, stride=cols), :
                ].astype(jnp.bfloat16)

    take_column(cols - 1)
    take_column(0)

    heard = 1 + jnp.logical_not(first).astype(jnp.int32)
    pl.semaphore_wait(barrier, heard + has_above.astype(jnp.int32) + has_below.astype(jnp.int32))

    @pl.when(last)
    def _():
        pl.semaphore_signal(wrap_sem, inc=1, device_id=east, device_id_type=MESH)

    def remote(src, dst, slot, device):
        return pltpu.make_async_remote_copy(
            src_ref=src,
            dst_ref=dst,
            send_sem=send_sem.at[slot],
            recv_sem=recv_sem.at[slot],
            device_id=device,
            device_id_type=MESH,
        )

    spans = [(0, mid_lo), (mid_hi, slots), (mid_lo, mid_hi)]
    to_east, to_west = [], []
    for i, (lo, hi) in enumerate(spans):
        span = pl.ds(lo, hi - lo)
        held = pl.ds(HALO + lo, hi - lo)
        to_east.append(remote(comb.at[cols, held], west_in.at[span], i, east))
        to_west.append(remote(comb.at[1, held], east_in.at[span], 3 + i, west))
    up = remote(comb.at[pl.ds(1, cols), pl.ds(HALO, HALO)], bot_in, 6, above)
    down = remote(tail, top_in, 7, below)
    head = pl.ds(0, HALO)
    up_w = remote(west_in.at[head], bot_w, 8, above)
    up_e = remote(east_in.at[head], bot_e, 9, above)
    down_w = remote(tail_w, top_w, 10, below)
    down_e = remote(tail_e, top_e, 11, below)

    @pl.when(last)
    def _():
        for copy in to_east + to_west:
            copy.start()

    @pl.when(jnp.logical_not(last | first))
    def _():
        for copy in to_west + to_east:
            copy.start()

    @pl.when(first)
    def _():
        for copy in to_east:
            copy.start()

    for x in range(1, cols - 1):
        take_column(x)

    @pl.when(has_above)
    def _():
        up.start()

    loads[1].wait()
    loads[2].wait()

    start_in = in_b[lat]
    end_in = in_b[lat + 1]
    count = end_in - start_in
    shift = 2 * out_b[lat] - start_in
    past = count - shift + 4

    for x in range(cols):
        for i in range(HALO):
            tail[x, i] = comb[1 + x, count + i]

    @pl.when(has_below)
    def _():
        down.start()

    for load in loads[3:]:
        load.wait()

    def place(r):
        inside = jnp.maximum(r + shift - 1, 0)
        outside = jnp.minimum(HALO + slots + r - past, total - 1)
        return jnp.where(r < past, inside, outside)

    spots = [place(r) for r in range(rows)]

    for e in range(2):
        for row, ref in ((0, dg_ref), (1, db_ref)):
            vec = ref[...][None]
            cuts = [vec[:, at : at + size] for which, at, size in down_pieces(chan) if which == e]
            down_vec[2 * e + row : 2 * e + row + 1, :] = jnp.concatenate(cuts, axis=1)
    for row, ref in ((0, ug_ref), (1, ub_ref)):
        vec = ref[...][None]
        up_vec[row : row + 1, :] = jnp.concatenate([vec, vec], axis=1)
    ow_pad[...] = jnp.zeros(ow_pad.shape, jnp.bfloat16)
    plain = ow[...]
    moved = jnp.concatenate([jnp.zeros((chan, short), jnp.bfloat16), plain], axis=1)
    for a in range(2):
        ow_pad[0, a, a * short : a * short + chan, 0:chan] = plain
        ow_pad[1, a, a * short : a * short + chan, :] = moved

    pairs_of_levels = LANES_OF_LEVELS // 2

    def compute(j, ms):
        nm = len(ms)
        part = nm * sub
        size = pairs_of_levels * part
        for k in range(0, nm, 2):
            for p in range(pairs_of_levels):
                cut = slice(p * 2 * chan, (p + 1) * 2 * chan)
                blocks = []
                for c in range(2):
                    for a in range(2):
                        rows_at = [comb[2 * j + c, spots[2 * m + a], :, cut] for m in ms[k : k + 2]]
                        blocks.append(thirds(jnp.concatenate([v.astype(jnp.float32) for v in rows_at], axis=0)))
                low, done = pair_norm(blocks, 4 * chan)
                even, odd = [v[0] for v in done], [v[2] for v in done]
                for b in (0, 2):
                    swapped = pltpu.roll(done[b + 1][1], TILE // 2, 1)
                    even.append(jnp.where(low, done[b][1], swapped))
                    odd.append(jnp.where(low, swapped, done[b][1]))
                for e, tiles_of in ((0, even), (1, odd)):
                    at = p * part + k * sub
                    for t, value in enumerate(tiles_of):
                        lane = slice(t * TILE, (t + 1) * TILE)
                        value = value * down_vec[2 * e : 2 * e + 1, lane] + down_vec[2 * e + 1 : 2 * e + 2, lane]
                        nrm[e, at : at + 2 * sub, lane] = value.astype(jnp.bfloat16)
        for e in range(2):
            wide = jnp.dot(nrm[e, 0:size, :], dw[e], preferred_element_type=jnp.float32)
            coarse[e * size : (e + 1) * size, :] = wide.astype(jnp.bfloat16)
            if j < 2:
                for i, m in enumerate(ms):
                    if m < 2:
                        continue
                    for p in range(pairs_of_levels):
                        at = p * part + i * sub
                        for t in range(2 * chan // TILE):
                            turn_merged[
                                m - 2, (2 * p + e) * 2 * chan // TILE + t, pl.ds(j, sub, stride=cols // 2), :
                            ] = wide[at : at + sub, t * TILE : (t + 1) * TILE]
        for c, x in (((1, 0),), ((0, 1), (1, 2)), ((0, 3),))[j]:
            spread = jnp.dot(
                coarse[0 : 2 * size, :],
                uw[:, c * 2 * chan : (c + 1) * 2 * chan],
                preferred_element_type=jnp.float32,
            )
            for at in range(0, 2 * size, 2 * sub):
                _, done = pair_norm([thirds(spread[at : at + 2 * sub])], chan)
                for t, value in enumerate(done[0]):
                    lane = slice(t * TILE, (t + 1) * TILE)
                    value = value * up_vec[0:1, lane] + up_vec[1:2, lane]
                    renorm[at : at + 2 * sub, lane] = value.astype(jnp.bfloat16)
            for a in range(2):
                two = [
                    jnp.dot(
                        renorm[e * size : (e + 1) * size, a * TILE : (a + 2) * TILE],
                        ow_pad[e, a],
                        preferred_element_type=jnp.float32,
                    )
                    for e in range(2)
                ]
                for i, m in enumerate(ms):
                    for p in range(pairs_of_levels):
                        span = slice(p * part + i * sub, p * part + (i + 1) * sub)
                        trio = (
                            two[0][span, 0:TILE],
                            two[0][span, TILE : 2 * TILE] + two[1][span, 0:TILE],
                            two[1][span, TILE : 2 * TILE],
                        )
                        for t, value in enumerate(trio):
                            turn_fine[2 * m + a, 3 * p + t, pl.ds(x, sub, stride=cols), :] = value

    own = pl.ds(1, cols)

    @pl.when(has_above)
    def _():
        down.wait_recv()

    @pl.when(has_below)
    def _():
        up.wait_recv()
        comb[own, HALO + slots : total] = bot_in[...]

    @pl.when(jnp.logical_not(has_below))
    def _():
        comb[:, HALO + slots : total] = jnp.zeros((cols + 2, HALO, sub, lanes), jnp.bfloat16)

    @pl.when(has_above)
    def _():
        comb[own, 0:HALO] = top_in[...]

    @pl.when(jnp.logical_not(has_above))
    def _():
        comb[:, 0:HALO] = jnp.zeros((cols + 2, HALO, sub, lanes), jnp.bfloat16)

    merged_rows = rows // 2
    with jax.named_scope("s_c1"):
        compute(1, list(range(merged_rows)))

    @pl.when(first)
    def _():
        pl.semaphore_wait(wrap_sem, 1)
        for copy in to_west:
            copy.start()

    def arrive(copies, landed, x, tail_x, up_x, down_x, top_x, bot_x):
        for i in range(2):
            lo, hi = spans[i]
            copies[i].wait_recv()
            comb[x, HALO + lo : HALO + hi] = landed[lo:hi]
        for i in range(HALO):
            tail_x[i] = comb[x, count + i]

        @pl.when(has_above)
        def _():
            up_x.start()

        @pl.when(has_below)
        def _():
            down_x.start()

        lo, hi = spans[2]
        copies[2].wait_recv()
        comb[x, HALO + lo : HALO + hi] = landed[lo:hi]

    def corners(x, up_x, down_x, top_x, bot_x):
        @pl.when(has_above)
        def _():
            down_x.wait_recv()
            comb[x, 0:HALO] = top_x[...]

        @pl.when(has_below)
        def _():
            up_x.wait_recv()
            comb[x, HALO + slots : total] = bot_x[...]

    with jax.named_scope("s_aW"):
        arrive(to_west, east_in, cols + 1, tail_e, up_e, down_e, top_e, bot_e)
    with jax.named_scope("s_cW"):
        corners(cols + 1, up_e, down_e, top_e, bot_e)
    with jax.named_scope("s_c2"):
        compute(2, list(range(merged_rows)))
    with jax.named_scope("s_aE"):
        arrive(to_east, west_in, 0, tail_w, up_w, down_w, top_w, bot_w)
    with jax.named_scope("s_cE"):
        corners(0, up_w, down_w, top_w, bot_w)

    def put_out(value, live, slot, out_ref, width, span):
        value = jnp.where(live, value, 0.0).astype(jnp.bfloat16)
        for half in range(halves):
            for member in range(members):
                at = (half * members + member) * width
                out_ref[member, slot, :, half * span : (half + 1) * span] = jnp.concatenate(
                    [value[t, at : at + width] for t in range(span // TILE)], axis=1
                )

    with jax.named_scope("s_c0"):
        compute(0, list(range(merged_rows)))
    count_out = out_b[lat + 1] - out_b[lat]
    for m in range(merged_slots):
        put_out(turn_merged[m], m < count_out, m, mo_ref, cols // 2, 2 * lanes)
    for k in range(slots):
        put_out(turn_fine[4 - shift + k], k < count, k, fo_ref, cols, lanes)

    for copy in to_east + to_west:
        copy.wait_send()

    @pl.when(has_above)
    def _():
        up.wait_send()
        up_w.wait_send()
        up_e.wait_send()

    @pl.when(has_below)
    def _():
        down.wait_send()
        down_w.wait_send()
        down_e.wait_send()


def write_out(merged_ref, fine_ref, merged_hbm, fine_hbm, sem):
    copies = [
        pltpu.make_async_copy(merged_ref, merged_hbm, sem.at[0]),
        pltpu.make_async_copy(fine_ref, fine_hbm, sem.at[1]),
    ]
    for copy in copies:
        copy.start()
    for copy in copies:
        copy.wait()


def body(
    tokens,
    in_bounds,
    out_bounds,
    down_gain,
    down_bias,
    down_weight,
    up_weight,
    up_gain,
    up_bias,
    out_weight,
):
    members, slots, cols, packed = tokens.shape
    chan = down_weight.shape[0] // 4
    halves = packed // (chan * LANES_OF_LEVELS)
    lanes = chan * LANES_OF_LEVELS
    sub = halves * members
    merged_slots = slots // 2 + 1
    half_cols = cols // 2
    rows = 2 * merged_slots + 4
    total = slots + 2 * HALO
    bf16 = jnp.bfloat16
    n_lat = lax.axis_size("lat")
    n_lon = lax.axis_size("lon")
    vmem = pl.BlockSpec(memory_space=pltpu.VMEM)
    hbm = pl.BlockSpec(memory_space=pltpu.HBM)
    column = pltpu.VMEM((slots, sub, lanes), bf16)
    patch = pltpu.VMEM((cols, HALO, sub, lanes), bf16)
    corner = pltpu.VMEM((HALO, sub, lanes), bf16)
    operands = (
        in_bounds,
        out_bounds,
        tokens,
        down_weight,
        up_weight,
        out_weight,
        down_gain,
        down_bias,
        up_gain,
        up_bias,
    )
    merged_shape = (members, merged_slots, half_cols, 2 * packed)
    held = pl.pallas_call(
        functools.partial(kernel, n_lat, n_lon),
        out_shape=(pltpu.VMEM(merged_shape, bf16), pltpu.VMEM(tokens.shape, bf16)),
        in_specs=[hbm] * 10,
        out_specs=(vmem, vmem),
        scratch_shapes=[
            pltpu.VMEM((cols + 2, total, sub, lanes), bf16),
            column,
            column,
            patch,
            patch,
            corner,
            corner,
            corner,
            corner,
            patch,
            corner,
            corner,
            pltpu.VMEM((2, LANES_OF_LEVELS * rows // 4 * sub, 4 * chan), bf16),
            pltpu.VMEM((LANES_OF_LEVELS * rows // 2 * sub, 2 * chan), bf16),
            pltpu.VMEM((LANES_OF_LEVELS * rows // 2 * sub, 2 * chan), bf16),
            pltpu.VMEM((slots, lanes // TILE, sub * cols, TILE), jnp.float32),
            pltpu.VMEM((merged_slots, 2 * lanes // TILE, sub * half_cols, TILE), jnp.float32),
            pltpu.VMEM((rows, lanes // TILE, sub * cols, TILE), jnp.float32),
            pltpu.VMEM((2, *down_weight.shape), bf16),
            pltpu.VMEM(up_weight.shape, bf16),
            pltpu.VMEM(out_weight.shape, bf16),
            pltpu.VMEM((2, 2, 2 * TILE, 2 * TILE), bf16),
            pltpu.VMEM((4, 4 * chan), jnp.float32),
            pltpu.VMEM((2, 2 * chan), jnp.float32),
            pltpu.VMEM(tokens.shape, bf16),
            pltpu.SMEM(in_bounds.shape, jnp.int32),
            pltpu.SMEM(out_bounds.shape, jnp.int32),
            pltpu.VMEM(down_gain.shape, jnp.float32),
            pltpu.VMEM(down_bias.shape, jnp.float32),
            pltpu.VMEM(up_gain.shape, jnp.float32),
            pltpu.VMEM(up_bias.shape, jnp.float32),
            pltpu.SemaphoreType.DMA((9 + len(down_pieces(chan)),)),
            pltpu.SemaphoreType.DMA((12,)),
            pltpu.SemaphoreType.DMA((12,)),
            pltpu.SemaphoreType.REGULAR,
        ],
        compiler_params=pltpu.CompilerParams(
            collective_id=0, has_side_effects=True, vmem_limit_bytes=48 * 2**20
        ),
    )(*[pltpu.with_memory_space_constraint(x, pltpu.HBM) for x in operands])
    return pl.pallas_call(
        write_out,
        out_shape=(
            jax.ShapeDtypeStruct(merged_shape, bf16),
            jax.ShapeDtypeStruct(tokens.shape, bf16),
        ),
        in_specs=[vmem, vmem],
        out_specs=(hbm, hbm),
        scratch_shapes=[pltpu.SemaphoreType.DMA((2,))],
    )(*[pltpu.with_memory_space_constraint(x, pltpu.VMEM) for x in held])


def solution(mesh):
    return jax.shard_map(
        body,
        mesh=mesh,
        in_specs=(P(None, "lat", "lon", None), P(), P(), P(), P(), P(), P(), P(), P(), P()),
        out_specs=(P(None, "lat", "lon", None), P(None, "lat", "lon", None)),
        check_vma=False,
    )
```

time: 27.5 us -> 21 us (0.76)
  Pallas kernels: 23.5 us -> 20.2 us
  local copies, waits for them, and re-layouts: 2.93 us -> 0 us
    pallas_call x1 -> x2, Pallas kernels: 23.5 us -> 20.2 us  [the longest x1 19.2 us: body(): pl.pallas_call(functools.partial(kernel, n_lat, n_lon), out_shape=(pltpu....]
    unnamed x4 -> x0, local copies, waits for them, and re-layouts: 2.93 us -> none
where the time goes in v1:
time: 21 us; the launch traced here: 20.8 us
  Pallas kernels  20.2 us (96%)
  between operations  0.64 us (3%)
    pallas_call x1, Pallas kernels, body(): pl.pallas_call(functools.partial(kernel, n_lat, n_lon), out_shape=(pltpu....  19.2 us
    pallas_call x1, Pallas kernels, body(): pl.pallas_call(write_out, out_shape=(jax.ShapeDtypeStruct(merged_shape, b...  1 us

profile of v1, /device:TPU:0, one launch (start us, length us, event | category | flops | bytes accessed | tf_op | source)
XLA Modules:
  0.0 20.8 jit_solution(8982455040192609168)
XLA Ops:
  0.6 19.2 %shard_map.113 = (bf16[4,8,2,3072]{3,2,1,0:T(2,128)(2,1)S(1)}, bf16[4,14,4,1536]{3,2,1,0:T(4,128)(2,1)S(1)}) custom-call(s32[5]{0:T(128)} %in_b_hbm.1, s32[5]{0:T(128)} %out_b_hbm.1, bf16[4,14,4,1536]{3,2,1,0:T(4,128)(2,1)} %t_hbm.1, bf16[768,384]{1,0:T(8,128)(2,1)} %dw_hbm.1, bf16[384,768]{1,0:T(8,128)(2,1)} %uw_hbm.1, bf16[192,192]{1,0:T(8,128)(2,1)} %ow_hbm.1, ...), custom_call_target="tpu_custom_call" | custom-call | tf_op jit(solution)/shard_map/pallas_call | solution.py:499
  19.8 1.0 %shard_map.114 = (bf16[4,8,2,3072]{3,2,1,0:T(2,128)(2,1)}, bf16[4,14,4,1536]{3,2,1,0:T(4,128)(2,1)}) custom-call(bf16[4,8,2,3072]{3,2,1,0:T(2,128)(2,1)S(1)} %get-tuple-element.4.merged_ref, bf16[4,14,4,1536]{3,2,1,0:T(4,128)(2,1)S(1)} %get-tuple-element.5.fine_ref), custom_call_target="tpu_custom_call" | custom-call | tf_op jit(solution)/shard_map/pallas_call | solution.py:545

commit v2 on v1

v2 whole, which is shorter than its diff:
```python
import functools

import jax
import jax.numpy as jnp
from jax import lax
from jax.experimental import pallas as pl
from jax.experimental.pallas import tpu as pltpu
from jax.sharding import PartitionSpec as P

HALO = 3
LANES_OF_LEVELS = 4
PAIRS = LANES_OF_LEVELS // 2
TILE = 128
TOP = 2
BOTTOM = 2
WEST, EAST = 0, 1
MESH = pl.DeviceIdType.MESH
F32 = jnp.float32
BF16 = jnp.bfloat16


def pair_norm(blocks, size):
    low = lax.broadcasted_iota(jnp.int32, blocks[0][0].shape, 1) < TILE // 2
    inv = 1.0 / size

    def totals(tiles):
        one, mid, two = [functools.reduce(jnp.add, group) for group in zip(*tiles)]
        first = jnp.sum(one + jnp.where(low, mid, 0.0), axis=1, keepdims=True) * inv
        second = jnp.sum(two + jnp.where(low, 0.0, mid), axis=1, keepdims=True) * inv
        return first, second

    first, second = totals(blocks)
    mid = jnp.where(low, first, second)
    off = [(one - first, both - mid, two - second) for one, both, two in blocks]
    first, second = totals([tuple(v * v for v in tiles) for tiles in off])
    first, second = lax.rsqrt(first + 1e-05), lax.rsqrt(second + 1e-05)
    mid = jnp.where(low, first, second)
    return low, [(one * first, both * mid, two * second) for one, both, two in off]


def thirds(value):
    return tuple(value[:, t * TILE : (t + 1) * TILE] for t in range(3))


def down_pieces(chan):
    short = chan - TILE
    even = [(0, b * chan, TILE) for b in range(4)] + [(0, b * chan + TILE, short) for b in range(4)]
    odd = [(1, b * chan + short, TILE) for b in range(4)] + [(1, b * chan, short) for b in (1, 0, 3, 2)]
    return even + odd


def kernel(
    n_lat,
    n_lon,
    in_b_hbm,
    out_b_hbm,
    t_hbm,
    dw_hbm,
    uw_hbm,
    ow_hbm,
    dg_hbm,
    db_hbm,
    ug_hbm,
    ub_hbm,
    turn_merged,
    turn_fine,
    places,
    comb,
    land,
    top_in,
    bot_in,
    top_side,
    bot_side,
    tail,
    tail_side,
    nrm,
    coarse,
    renorm,
    turn_in,
    dw,
    uw,
    ow,
    ow_pad,
    down_vec,
    up_vec,
    t_ref,
    in_b,
    out_b,
    dg_ref,
    db_ref,
    ug_ref,
    ub_ref,
    local_sem,
    send_sem,
    recv_sem,
    wrap_sem,
):
    members, slots, cols, packed = t_ref.shape
    _, _, sub, lanes = comb.shape
    halves = sub // members
    chan = lanes // LANES_OF_LEVELS
    short = chan - TILE
    tiles = lanes // TILE
    total = slots + 2 * HALO
    half_cols = cols // 2
    inner = slots // 2
    mid_lo, mid_hi = HALO, slots // 2
    lat = lax.axis_index("lat")
    lon = lax.axis_index("lon")
    east = {"lat": lat, "lon": lax.rem(lon + 1, n_lon)}
    west = {"lat": lat, "lon": lax.rem(lon + n_lon - 1, n_lon)}
    above = {"lat": jnp.maximum(lat - 1, 0), "lon": lon}
    below = {"lat": jnp.minimum(lat + 1, n_lat - 1), "lon": lon}
    has_above = lat > 0
    has_below = lat < n_lat - 1
    first = lon == 0
    last = lon == n_lon - 1

    barrier = pltpu.get_barrier_semaphore()
    pl.semaphore_signal(barrier, inc=1, device_id=west, device_id_type=MESH)

    @pl.when(jnp.logical_not(last))
    def _():
        pl.semaphore_signal(barrier, inc=1, device_id=east, device_id_type=MESH)

    @pl.when(has_above)
    def _():
        pl.semaphore_signal(barrier, inc=1, device_id=above, device_id_type=MESH)

    @pl.when(has_below)
    def _():
        pl.semaphore_signal(barrier, inc=1, device_id=below, device_id_type=MESH)

    pairs = [
        (t_hbm, t_ref),
        (in_b_hbm, in_b),
        (out_b_hbm, out_b),
        (ow_hbm, ow),
        (dg_hbm, dg_ref),
        (db_hbm, db_ref),
        (ug_hbm, ug_ref),
        (ub_hbm, ub_ref),
    ]
    loads = [pltpu.make_async_copy(src, dst, local_sem.at[i]) for i, (src, dst) in enumerate(pairs)]
    for load in loads:
        load.start()
    for block in range(2):
        cut = uw_hbm.at[:, pl.ds(block * 2 * chan, 2 * chan)]
        pltpu.make_async_copy(cut, uw.at[block], local_sem.at[len(pairs)]).start()
    for pos, (e, start, size) in enumerate(down_pieces(chan)):
        at = sum(piece[2] for piece in down_pieces(chan)[:pos] if piece[0] == e)
        cut = dw_hbm.at[pl.ds(start, size)]
        pltpu.make_async_copy(cut, dw.at[e, pl.ds(at, size)], local_sem.at[len(pairs) + 1]).start()
    loads[0].wait()

    for r in range(slots):
        for member in range(members):
            row = t_ref[member, r].astype(F32)
            for half in range(halves):
                at = (half * members + member) * cols
                for t in range(tiles):
                    lane = half * lanes + t * TILE
                    turn_in[r, t, at : at + cols, :] = row[:, lane : lane + TILE]

    for x in range(cols):
        for r in range(slots):
            for t in range(tiles):
                comb[1 + x, HALO + r, :, t * TILE : (t + 1) * TILE] = turn_in[
                    r, t, pl.ds(x, sub, stride=cols), :
                ].astype(BF16)

    loads[1].wait()
    loads[2].wait()
    start_in = in_b[lat]
    count = in_b[lat + 1] - start_in
    shift = 2 * out_b[lat] - start_in
    past = count - shift + 2 * TOP
    edge = past // 2
    places[0] = count
    places[1] = shift
    places[2] = edge
    places[3] = out_b[lat + 1] - out_b[lat]
    for x in range(cols):
        for i in range(HALO):
            tail[x, i] = comb[1 + x, count + i]

    heard = 1 + jnp.logical_not(first).astype(jnp.int32)
    pl.semaphore_wait(barrier, heard + has_above.astype(jnp.int32) + has_below.astype(jnp.int32))

    @pl.when(last)
    def _():
        pl.semaphore_signal(wrap_sem, inc=1, device_id=east, device_id_type=MESH)

    def remote(src, dst, slot, device):
        return pltpu.make_async_remote_copy(
            src_ref=src,
            dst_ref=dst,
            send_sem=send_sem.at[slot],
            recv_sem=recv_sem.at[slot],
            device_id=device,
            device_id_type=MESH,
        )

    spans = [(0, mid_lo), (mid_hi, slots), (mid_lo, mid_hi)]

    def column(side, x, i, device):
        lo, hi = spans[i]
        span = pl.ds(lo, hi - lo)
        return remote(comb.at[x, pl.ds(HALO + lo, hi - lo)], land.at[side, span], 3 * side + i, device)

    to_east = [column(WEST, cols, i, east) for i in range(3)]
    to_west = [column(EAST, 1, i, west) for i in range(3)]
    up = remote(comb.at[pl.ds(1, cols), pl.ds(HALO, HALO)], bot_in, 6, above)
    down = remote(tail, top_in, 7, below)

    def up_side(side):
        return remote(land.at[side, pl.ds(0, HALO)], bot_side.at[side], 8 + side, above)

    def down_side(side):
        return remote(tail_side.at[side], top_side.at[side], 10 + side, below)

    @pl.when(has_above)
    def _():
        up.start()

    @pl.when(has_below)
    def _():
        down.start()

    @pl.when(jnp.logical_not(last))
    def _():
        for copy in to_east:
            copy.start()

    @pl.when(jnp.logical_not(first))
    def _():
        for copy in to_west:
            copy.start()

    for load in loads[3:]:
        load.wait()
    pltpu.make_async_copy(uw, uw, local_sem.at[len(pairs)]).wait()
    pltpu.make_async_copy(dw, dw, local_sem.at[len(pairs) + 1]).wait()

    for e in range(2):
        for row, ref in ((0, dg_ref), (1, db_ref)):
            vec = ref[...][None]
            cuts = [vec[:, at : at + size] for which, at, size in down_pieces(chan) if which == e]
            down_vec[2 * e + row : 2 * e + row + 1, :] = jnp.concatenate(cuts, axis=1)
    for row, ref in ((0, ug_ref), (1, ub_ref)):
        vec = ref[...][None]
        up_vec[row : row + 1, :] = jnp.concatenate([vec, vec], axis=1)
    ow_pad[...] = jnp.zeros(ow_pad.shape, BF16)
    plain = ow[...]
    moved = jnp.concatenate([jnp.zeros((chan, short), BF16), plain], axis=1)
    for a in range(2):
        ow_pad[0, a, a * short : a * short + chan, 0:chan] = plain
        ow_pad[1, a, a * short : a * short + chan, :] = moved

    turn_fine[2 * (TOP + inner + BOTTOM)] = jnp.zeros(turn_fine.shape[1:], F32)
    turn_merged[inner + BOTTOM] = jnp.zeros(turn_merged.shape[1:], F32)

    def place(r):
        inside = jnp.maximum(r + shift - 1, 0)
        outside = jnp.minimum(HALO + slots + r - past, total - 1)
        return jnp.where(r < past, inside, outside)

    top_rows = [([place(2 * m + a) for a in range(2)], 2 * m, None) for m in range(TOP)]
    inner_rows = [([2 * m + a + shift - 1 for a in range(2)], 2 * m, m - TOP) for m in range(TOP, TOP + inner)]
    bottom_rows = [
        ([place(2 * (edge + i) + a) for a in range(2)], 2 * (TOP + inner + i), inner + i) for i in range(BOTTOM)
    ]
    step = PAIRS * sub

    def compute(cells, ups, skip=0):
        n = len(cells)
        size = n * step
        groups = sorted({(lo, hi) for lo, hi, _, _ in ups})

        def coarse_at(i, e):
            lo, hi = next(group for group in groups if group[0] <= i < group[1])
            return 2 * lo * step + e * (hi - lo) * step + (i - lo) * step

        for i, (col, _, (spots, _, _)) in enumerate(cells):
            blocks = []
            for c in range(2):
                for a in range(2):
                    row = comb[col + c, spots[a]].astype(F32)
                    both = [row[:, p * 2 * chan : (p + 1) * 2 * chan] for p in range(PAIRS)]
                    blocks.append(thirds(jnp.concatenate(both, axis=0)))
            low, done = pair_norm(blocks, 4 * chan)
            even, odd = [v[0] for v in done], [v[2] for v in done]
            for b in (0, 2):
                swapped = pltpu.roll(done[b + 1][1], TILE // 2, 1)
                even.append(jnp.where(low, done[b][1], swapped))
                odd.append(jnp.where(low, swapped, done[b][1]))
            for e, values in ((0, even), (1, odd)):
                for t, value in enumerate(values):
                    lane = slice(t * TILE, (t + 1) * TILE)
                    value = value * down_vec[2 * e : 2 * e + 1, lane] + down_vec[2 * e + 1 : 2 * e + 2, lane]
                    nrm[e, i * step : (i + 1) * step, lane] = value.astype(BF16)
        for e in range(2):
            wide = jnp.dot(nrm[e, 0:size, :], dw[e], preferred_element_type=F32)
            narrow = wide.astype(BF16)
            for i, (_, merged_col, (_, _, merged_at)) in enumerate(cells):
                coarse[coarse_at(i, e) : coarse_at(i, e) + step, :] = narrow[i * step : (i + 1) * step]
                if merged_col is None or merged_at is None:
                    continue
                for p in range(PAIRS):
                    at = i * step + p * sub
                    for t in range(3):
                        turn_merged[
                            merged_at + skip, (2 * p + e) * 3 + t, pl.ds(merged_col, sub, stride=half_cols), :
                        ] = wide[at : at + sub, t * TILE : (t + 1) * TILE]
        whole = sum(hi - lo for lo, hi, _, _ in ups) * step
        off = 0
        offs = []
        for lo, hi, block, _ in ups:
            part = (hi - lo) * step
            spread = jnp.dot(coarse[2 * lo * step : 2 * hi * step, :], uw[block], preferred_element_type=F32)
            for e in range(2):
                for at in range(0, part, step):
                    _, done = pair_norm([thirds(spread[e * part + at : e * part + at + step])], chan)
                    for t, value in enumerate(done[0]):
                        lane = slice(t * TILE, (t + 1) * TILE)
                        value = value * up_vec[0:1, lane] + up_vec[1:2, lane]
                        renorm[e * whole + off + at : e * whole + off + at + step, lane] = value.astype(BF16)
            offs.append(off)
            off += part
        for a in range(2):
            two = [
                jnp.dot(
                    renorm[e * whole : (e + 1) * whole, a * TILE : (a + 2) * TILE],
                    ow_pad[e, a],
                    preferred_element_type=F32,
                )
                for e in range(2)
            ]
            for (lo, hi, _, x), off in zip(ups, offs):
                for i in range(lo, hi):
                    _, _, (_, fine_at, _) = cells[i]
                    for p in range(PAIRS):
                        at = off + (i - lo) * step + p * sub
                        span = slice(at, at + sub)
                        trio = (
                            two[0][span, 0:TILE],
                            two[0][span, TILE : 2 * TILE] + two[1][span, 0:TILE],
                            two[1][span, TILE : 2 * TILE],
                        )
                        for t, value in enumerate(trio):
                            turn_fine[fine_at + a, 3 * p + t, pl.ds(x, sub, stride=cols), :] = value

    own = pl.ds(1, cols)

    with jax.named_scope("c_own_inner"):
        compute([(2, 1, row) for row in inner_rows], [(0, inner, 0, 1), (0, inner, 1, 2)])

    @pl.when(last)
    def _():
        for copy in to_east:
            copy.start()

    with jax.named_scope("w_halo"):

        @pl.when(has_above)
        def _():
            down.wait_recv()

        @pl.when(has_below)
        def _():
            up.wait_recv()
            comb[own, HALO + slots : total] = bot_in[...]

        @pl.when(jnp.logical_not(has_below))
        def _():
            comb[:, HALO + slots : total] = jnp.zeros((cols + 2, HALO, sub, lanes), BF16)

        @pl.when(has_above)
        def _():
            comb[own, 0:HALO] = top_in[...]

        @pl.when(jnp.logical_not(has_above))
        def _():
            comb[:, 0:HALO] = jnp.zeros((cols + 2, HALO, sub, lanes), BF16)

    with jax.named_scope("w_wrap"):

        @pl.when(first)
        def _():
            pl.semaphore_wait(wrap_sem, 1)
            for copy in to_west:
                copy.start()

    cross_lo = has_above & (lax.rem(lat, 2) == 0)
    cross_hi = has_below & (lax.rem(lat, 2) == 1)
    wrap_top_send = pltpu.make_async_remote_copy(
        src_ref=top_in.at[cols - 1],
        dst_ref=top_side.at[WEST],
        send_sem=send_sem.at[12],
        recv_sem=recv_sem.at[10 + WEST],
        device_id=east,
        device_id_type=MESH,
    )
    wrap_bot_send = pltpu.make_async_remote_copy(
        src_ref=bot_in.at[cols - 1],
        dst_ref=bot_side.at[WEST],
        send_sem=send_sem.at[12],
        recv_sem=recv_sem.at[8 + WEST],
        device_id=east,
        device_id_type=MESH,
    )

    @pl.when(last & cross_lo)
    def _():
        wrap_top_send.start()

    @pl.when(last & cross_hi)
    def _():
        wrap_bot_send.start()

    outer = top_rows + bottom_rows
    edges = len(outer)
    with jax.named_scope("c_own_outer"):
        compute([(2, 1, row) for row in outer], [(0, edges, 0, 1), (0, edges, 1, 2)])

    odd = lax.rem(lon, 2) == 1
    side_one = jnp.where(first | (odd & jnp.logical_not(last)), EAST, WEST)
    side_two = 1 - side_one

    def arrive(side):
        x = side * (cols + 1)
        for i in range(2):
            lo, hi = spans[i]
            column(side, cols, i, east).wait_recv()
            comb[x, HALO + lo : HALO + hi] = land[side, lo:hi]
        for i in range(HALO):
            tail_side[side, i] = comb[x, count + i]

        skip = first & (side == WEST)

        @pl.when(has_above & jnp.logical_not(skip & cross_lo))
        def _():
            up_side(side).start()

        @pl.when(has_below & jnp.logical_not(skip & cross_hi))
        def _():
            down_side(side).start()

        lo, hi = spans[2]
        column(side, cols, 2, east).wait_recv()
        comb[x, HALO + lo : HALO + hi] = land[side, lo:hi]


    def corner(side):
        x = side * (cols + 1)

        @pl.when(has_above)
        def _():
            down_side(side).wait_recv()
            comb[x, 0:HALO] = top_side[side]

        @pl.when(has_below)
        def _():
            up_side(side).wait_recv()
            comb[x, HALO + slots : total] = bot_side[side]

    side_rows = top_rows + inner_rows + bottom_rows
    for name, side in (("one", side_one), ("two", side_two)):
        with jax.named_scope("w_" + name):
            arrive(side)
        with jax.named_scope("k_" + name):
            corner(side)
        with jax.named_scope("c_" + name):
            compute(
                [(side * cols, 0, row) for row in side_rows],
                [(0, len(side_rows), 1 - side, side * (cols - 1))],
                skip=side * (inner + BOTTOM + 1),
            )

    for copy in to_east + to_west:
        copy.wait_send()

    @pl.when(has_above)
    def _():
        up.wait_send()
        up_side(EAST).wait_send()

    @pl.when(has_below)
    def _():
        down.wait_send()
        down_side(EAST).wait_send()

    @pl.when(has_above & jnp.logical_not(first & cross_lo))
    def _():
        up_side(WEST).wait_send()

    @pl.when(has_below & jnp.logical_not(first & cross_hi))
    def _():
        down_side(WEST).wait_send()

    @pl.when(last & (cross_lo | cross_hi))
    def _():
        wrap_top_send.wait_send()


def write_out(turn_merged, turn_fine, places, merged_hbm, fine_hbm, merged_buf, fine_buf, sem):
    members, merged_slots, half_cols, _ = merged_buf.shape
    _, slots, cols, packed = fine_buf.shape
    sub = turn_fine.shape[2] // cols
    halves = sub // members
    lanes = packed // halves
    inner = slots // 2
    count, shift, edge, count_out = places[0], places[1], places[2], places[3]
    copies = []

    def put(turn, index, slot, buf, width, span):
        value = turn[index].astype(BF16)
        for half in range(halves):
            for member in range(members):
                at = (half * members + member) * width
                buf[member, slot, :, half * span : (half + 1) * span] = jnp.concatenate(
                    [value[t, at : at + width] for t in range(span // TILE)], axis=1
                )

    def send(buf, hbm, lo, hi):
        span = pl.ds(lo, hi - lo)
        copy = pltpu.make_async_copy(buf.at[:, span], hbm.at[:, span], sem.at[len(copies)])
        copy.start()
        copies.append(copy)

    for lo in range(0, merged_slots, 4):
        hi = min(lo + 4, merged_slots)
        for slot in range(lo, hi):
            m = slot + TOP
            index = jnp.where(m < edge, slot, jnp.minimum(inner + m - edge, inner + BOTTOM - 1))
            index = jnp.where(slot < count_out, index, inner + BOTTOM)
            put(turn_merged, index, slot, merged_buf, half_cols, 2 * lanes)
        send(merged_buf, merged_hbm, lo, hi)
    for lo in range(0, slots, 5):
        hi = min(lo + 5, slots)
        for slot in range(lo, hi):
            r = slot + 2 * TOP - shift
            after = jnp.minimum(2 * (TOP + inner) + r - 2 * edge, 2 * (TOP + inner + BOTTOM) - 1)
            index = jnp.where(r < 2 * edge, r, after)
            index = jnp.where(slot < count, index, 2 * (TOP + inner + BOTTOM))
            put(turn_fine, index, slot, fine_buf, cols, lanes)
        send(fine_buf, fine_hbm, lo, hi)
    for copy in copies:
        copy.wait()


def body(
    tokens,
    in_bounds,
    out_bounds,
    down_gain,
    down_bias,
    down_weight,
    up_weight,
    up_gain,
    up_bias,
    out_weight,
):
    members, slots, cols, packed = tokens.shape
    chan = down_weight.shape[0] // 4
    halves = packed // (chan * LANES_OF_LEVELS)
    lanes = chan * LANES_OF_LEVELS
    sub = halves * members
    merged_slots = slots // 2 + 1
    half_cols = cols // 2
    inner = slots // 2
    edges = TOP + BOTTOM
    total = slots + 2 * HALO
    most = (inner + edges) * PAIRS * sub
    wide = max(2 * inner, inner + edges) * PAIRS * sub
    n_lat = lax.axis_size("lat")
    n_lon = lax.axis_size("lon")
    vmem = pl.BlockSpec(memory_space=pltpu.VMEM)
    smem = pl.BlockSpec(memory_space=pltpu.SMEM)
    hbm = pl.BlockSpec(memory_space=pltpu.HBM)
    patch = pltpu.VMEM((cols, HALO, sub, lanes), BF16)
    corner = pltpu.VMEM((2, HALO, sub, lanes), BF16)
    operands = (
        in_bounds,
        out_bounds,
        tokens,
        down_weight,
        up_weight,
        out_weight,
        down_gain,
        down_bias,
        up_gain,
        up_bias,
    )
    merged_shape = (members, merged_slots, half_cols, 2 * packed)
    held = pl.pallas_call(
        functools.partial(kernel, n_lat, n_lon),
        out_shape=(
            pltpu.VMEM((2 * (inner + BOTTOM) + 1, 2 * lanes // TILE, half_cols * sub, TILE), F32),
            pltpu.VMEM((2 * (TOP + inner + BOTTOM) + 1, lanes // TILE, cols * sub, TILE), F32),
            pltpu.SMEM((4,), jnp.int32),
        ),
        in_specs=[hbm] * 10,
        out_specs=(vmem, vmem, smem),
        scratch_shapes=[
            pltpu.VMEM((cols + 2, total, sub, lanes), BF16),
            pltpu.VMEM((2, slots, sub, lanes), BF16),
            patch,
            patch,
            corner,
            corner,
            patch,
            corner,
            pltpu.VMEM((2, most, 4 * chan), BF16),
            pltpu.VMEM((2 * most, 2 * chan), BF16),
            pltpu.VMEM((2 * wide, 2 * chan), BF16),
            pltpu.VMEM((slots, lanes // TILE, sub * cols, TILE), F32),
            pltpu.VMEM((2, *down_weight.shape), BF16),
            pltpu.VMEM((2, 2 * chan, 2 * chan), BF16),
            pltpu.VMEM(out_weight.shape, BF16),
            pltpu.VMEM((2, 2, 2 * TILE, 2 * TILE), BF16),
            pltpu.VMEM((4, 4 * chan), F32),
            pltpu.VMEM((2, 2 * chan), F32),
            pltpu.VMEM(tokens.shape, BF16),
            pltpu.SMEM(in_bounds.shape, jnp.int32),
            pltpu.SMEM(out_bounds.shape, jnp.int32),
            pltpu.VMEM(down_gain.shape, F32),
            pltpu.VMEM(down_bias.shape, F32),
            pltpu.VMEM(up_gain.shape, F32),
            pltpu.VMEM(up_bias.shape, F32),
            pltpu.SemaphoreType.DMA((10,)),
            pltpu.SemaphoreType.DMA((13,)),
            pltpu.SemaphoreType.DMA((12,)),
            pltpu.SemaphoreType.REGULAR,
        ],
        compiler_params=pltpu.CompilerParams(
            collective_id=0, has_side_effects=True, vmem_limit_bytes=48 * 2**20
        ),
    )(*[pltpu.with_memory_space_constraint(x, pltpu.HBM) for x in operands])
    spaces = (pltpu.VMEM, pltpu.VMEM, pltpu.SMEM)
    return pl.pallas_call(
        write_out,
        out_shape=(
            jax.ShapeDtypeStruct(merged_shape, BF16),
            jax.ShapeDtypeStruct(tokens.shape, BF16),
        ),
        in_specs=[vmem, vmem, smem],
        out_specs=(hbm, hbm),
        scratch_shapes=[
            pltpu.VMEM(merged_shape, BF16),
            pltpu.VMEM(tokens.shape, BF16),
            pltpu.SemaphoreType.DMA((pl.cdiv(merged_slots, 4) + pl.cdiv(slots, 5),)),
        ],
        compiler_params=pltpu.CompilerParams(vmem_limit_bytes=48 * 2**20),
    )(*[pltpu.with_memory_space_constraint(x, space) for x, space in zip(held, spaces)])


def solution(mesh):
    return jax.shard_map(
        body,
        mesh=mesh,
        in_specs=(P(None, "lat", "lon", None), P(), P(), P(), P(), P(), P(), P(), P(), P()),
        out_specs=(P(None, "lat", "lon", None), P(None, "lat", "lon", None)),
        check_vma=False,
    )
```

time: 21 us -> 17.9 us (0.85)
  Pallas kernels: 20.2 us -> 17.1 us
    pallas_call x1, Pallas kernels: 19.2 us -> 16.1 us  [body(): pl.pallas_call(functools.partial(kernel, n_lat, n_lon), out_shape=(pltpu....]
where the time goes in v2:
time: 17.9 us; the launch traced here: 17.8 us
  Pallas kernels  17.1 us (96%)
  between operations  0.64 us (4%)
    pallas_call x1, Pallas kernels, body(): pl.pallas_call(functools.partial(kernel, n_lat, n_lon), out_shape=(pltpu....  16.1 us
    pallas_call x1, Pallas kernels, body(): pl.pallas_call(write_out, out_shape=(jax.ShapeDtypeStruct(merged_shape, B...  1.06 us

profile of v2, /device:TPU:0, one launch (start us, length us, event | category | flops | bytes accessed | tf_op | source)
XLA Modules:
  0.0 17.8 jit_solution(11350038711896267893)
XLA Ops:
  0.6 16.1 %shard_map.113 = (f32[19,12,16,128]{3,2,1,0:T(8,128)S(1)}, f32[23,6,32,128]{3,2,1,0:T(8,128)S(1)}, s32[4]{0:T(128)S(4)}) custom-call(s32[5]{0:T(128)} %in_b_hbm.1, s32[5]{0:T(128)} %out_b_hbm.1, bf16[4,14,4,1536]{3,2,1,0:T(4,128)(2,1)} %t_hbm.1, bf16[768,384]{1,0:T(8,128)(2,1)} %dw_hbm.1, bf16[384,768]{1,0:T(8,128)(2,1)} %uw_hbm.1, bf16[192,192]{1,0:T(8,128)(2,1)} %ow_hbm.1, ...), custom_call_target="tpu_custom_call" | custom-call | tf_op jit(solution)/shard_map/pallas_call | solution.py:596
  16.7 1.1 %shard_map.114 = (bf16[4,8,2,3072]{3,2,1,0:T(2,128)(2,1)}, bf16[4,14,4,1536]{3,2,1,0:T(4,128)(2,1)}) custom-call(f32[19,12,16,128]{3,2,1,0:T(8,128)S(1)} %get-tuple-element.5.turn_merged, f32[23,6,32,128]{3,2,1,0:T(8,128)S(1)} %get-tuple-element.6.turn_fine, s32[4]{0:T(128)S(4)} %get-tuple-element.7.places), custom_call_target="tpu_custom_call" | custom-call | tf_op jit(solution)/shard_map/pallas_call | solution.py:641

commit v3 on v2

--- a/solution.py
+++ b/solution.py
@@ -17,6 +17,7 @@
 MESH = pl.DeviceIdType.MESH
 F32 = jnp.float32
 BF16 = jnp.bfloat16
+PARITIES = ((0, 1),)
 
 
 def pair_norm(blocks, size):
@@ -93,7 +94,7 @@
     local_sem,
     send_sem,
     recv_sem,
-    wrap_sem,
+    ready_sem,
 ):
     members, slots, cols, packed = t_ref.shape
     _, _, sub, lanes = comb.shape
@@ -115,24 +116,30 @@
     has_below = lat < n_lat - 1
     first = lon == 0
     last = lon == n_lon - 1
+    before_last = lon == n_lon - 2
+
+    spans = [(0, mid_lo), (mid_hi, slots), (mid_lo, mid_hi)]
+    token_loads = []
+    for i, (lo, hi) in enumerate(spans):
+        span = pl.ds(lo, hi - lo)
+        token_loads.append(pltpu.make_async_copy(t_hbm.at[:, span], t_ref.at[:, span], local_sem.at[i]))
+        token_loads[i].start()
 
     barrier = pltpu.get_barrier_semaphore()
-    pl.semaphore_signal(barrier, inc=1, device_id=west, device_id_type=MESH)
+
+    @pl.when(first | last)
+    def _():
+        pl.semaphore_signal(barrier, inc=1, device_id=west, device_id_type=MESH)
 
     @pl.when(jnp.logical_not(last))
     def _():
         pl.semaphore_signal(barrier, inc=1, device_id=east, device_id_type=MESH)
 
-    @pl.when(has_above)
-    def _():
-        pl.semaphore_signal(barrier, inc=1, device_id=above, device_id_type=MESH)
-
     @pl.when(has_below)
     def _():
         pl.semaphore_signal(barrier, inc=1, device_id=below, device_id_type=MESH)
 
     pairs = [
-        (t_hbm, t_ref),
         (in_b_hbm, in_b),
         (out_b_hbm, out_b),
         (ow_hbm, ow),
@@ -141,36 +148,124 @@
         (ug_hbm, ug_ref),
         (ub_hbm, ub_ref),
     ]
-    loads = [pltpu.make_async_copy(src, dst, local_sem.at[i]) for i, (src, dst) in enumerate(pairs)]
+    loads = [pltpu.make_async_copy(src, dst, local_sem.at[3 + i]) for i, (src, dst) in enumerate(pairs)]
     for load in loads:
         load.start()
     for block in range(2):
         cut = uw_hbm.at[:, pl.ds(block * 2 * chan, 2 * chan)]
-        pltpu.make_async_copy(cut, uw.at[block], local_sem.at[len(pairs)]).start()
+        pltpu.make_async_copy(cut, uw.at[block], local_sem.at[3 + len(pairs)]).start()
     for pos, (e, start, size) in enumerate(down_pieces(chan)):
         at = sum(piece[2] for piece in down_pieces(chan)[:pos] if piece[0] == e)
         cut = dw_hbm.at[pl.ds(start, size)]
-        pltpu.make_async_copy(cut, dw.at[e, pl.ds(at, size)], local_sem.at[len(pairs) + 1]).start()
+        pltpu.make_async_copy(cut, dw.at[e, pl.ds(at, size)], local_sem.at[4 + len(pairs)]).start()
+
+    def take_rows(lo, hi):
+        for r in range(lo, hi):
+            for member in range(members):
+                row = t_ref[member, r].astype(F32)
+                for half in range(halves):
+                    at = (half * members + member) * cols
+                    for t in range(tiles):
+                        lane = half * lanes + t * TILE
+                        turn_in[r, t, at : at + cols, :] = row[:, lane : lane + TILE]
+        for x in range(cols):
+            for r in range(lo, hi):
+                for t in range(tiles):
+                    comb[1 + x, HALO + r, :, t * TILE : (t + 1) * TILE] = turn_in[
+                        r, t, pl.ds(x, sub, stride=cols), :
+                    ].astype(BF16)
+
+    heard = has_above.astype(jnp.int32) + jnp.logical_not(first).astype(jnp.int32)
+    heard = heard + last.astype(jnp.int32) + before_last.astype(jnp.int32)
+    @pl.when(heard > 0)
+    def _():
+        pl.semaphore_wait(barrier, heard)
+
+    @pl.when(jnp.logical_not(first | last))
+    def _():
+        pl.semaphore_signal(ready_sem.at[0], inc=1, device_id=west, device_id_type=MESH)
+
+    @pl.when(last)
+    def _():
+        pl.semaphore_signal(ready_sem.at[2], inc=1, device_id=east, device_id_type=MESH)
+
+    @pl.when(has_above)
+    def _():
+        pl.semaphore_signal(ready_sem.at[1], inc=1, device_id=above, device_id_type=MESH)
+
+    with jax.named_scope("w_tok"):
+        token_loads[0].wait()
+    take_rows(*spans[0])
+
+    def remote(src, dst, slot, device, landing=None):
+        return pltpu.make_async_remote_copy(
+            src_ref=src,
+            dst_ref=dst,
+            send_sem=send_sem.at[slot],
+            recv_sem=recv_sem.at[slot if landing is None else landing],
+            device_id=device,
+            device_id_type=MESH,
+        )
+
+    def column(side, x, i, device):
+        lo, hi = spans[i]
+        span = pl.ds(lo, hi - lo)
+        return remote(comb.at[x, pl.ds(HALO + lo, hi - lo)], land.at[side, span], side, device, 3 * side + i)
+
+    to_east = [column(WEST, cols, i, east) for i in range(3)]
+    to_west = [column(EAST, 1, i, west) for i in range(3)]
+    up = remote(comb.at[pl.ds(1, cols), pl.ds(HALO, HALO)], bot_in, 2, above, 6)
+    down = remote(tail, top_in, 3, below, 7)
+
+    def up_side(side):
+        return remote(land.at[side, pl.ds(0, HALO)], bot_side.at[side], 4 + side, above, 8 + side)
+
+    def down_side(side):
+        return remote(tail_side.at[side], top_side.at[side], 6 + side, below, 10 + side)
+
+    cross_lo = has_above & (lax.rem(lat, 2) == 0)
+    cross_hi = has_below & (lax.rem(lat, 2) == 1)
+
+    def sends_cross(side):
+        return jnp.where(side == WEST, lon != n_lon - 2, lon != 1)
+
+    def takes_cross(side):
+        return jnp.where(side == WEST, jnp.logical_not(last), jnp.logical_not(first))
+
+    def cross(side, x, device, held, landed, slot):
+        return pltpu.make_async_remote_copy(
+            src_ref=held.at[x],
+            dst_ref=landed.at[side],
+            send_sem=send_sem.at[8 + side],
+            recv_sem=recv_sem.at[slot + side],
+            device_id=device,
+            device_id_type=MESH,
+        )
+
+    def start_early(i):
+        @pl.when(before_last)
+        def _():
+            to_east[i].start()
+
+        @pl.when(jnp.logical_not(first))
+        def _():
+            to_west[i].start()
+
+    start_early(0)
+
+    @pl.when(has_above)
+    def _():
+        up.start()
+
+    token_loads[1].wait()
+    take_rows(*spans[1])
+    start_early(1)
+    token_loads[2].wait()
+    take_rows(*spans[2])
+    start_early(2)
+
     loads[0].wait()
-
-    for r in range(slots):
-        for member in range(members):
-            row = t_ref[member, r].astype(F32)
-            for half in range(halves):
-                at = (half * members + member) * cols
-                for t in range(tiles):
-                    lane = half * lanes + t * TILE
-                    turn_in[r, t, at : at + cols, :] = row[:, lane : lane + TILE]
-
-    for x in range(cols):
-        for r in range(slots):
-            for t in range(tiles):
-                comb[1 + x, HALO + r, :, t * TILE : (t + 1) * TILE] = turn_in[
-                    r, t, pl.ds(x, sub, stride=cols), :
-                ].astype(BF16)
-
     loads[1].wait()
-    loads[2].wait()
     start_in = in_b[lat]
     count = in_b[lat + 1] - start_in
     shift = 2 * out_b[lat] - start_in
@@ -184,63 +279,28 @@
         for i in range(HALO):
             tail[x, i] = comb[1 + x, count + i]
 
-    heard = 1 + jnp.logical_not(first).astype(jnp.int32)
-    pl.semaphore_wait(barrier, heard + has_above.astype(jnp.int32) + has_below.astype(jnp.int32))
+    with jax.named_scope("w_ready"):
+
+        @pl.when(jnp.logical_not(last | before_last))
+        def _():
+            pl.semaphore_wait(ready_sem.at[0], 1)
+            for copy in to_east:
+                copy.start()
+
+    @pl.when(has_below)
+    def _():
+        pl.semaphore_wait(ready_sem.at[1], 1)
+        down.start()
+
+    for load in loads[2:]:
+        load.wait()
+    pltpu.make_async_copy(uw, uw, local_sem.at[3 + len(pairs)]).wait()
+    pltpu.make_async_copy(dw, dw, local_sem.at[4 + len(pairs)]).wait()
 
     @pl.when(last)
-    def _():
-        pl.semaphore_signal(wrap_sem, inc=1, device_id=east, device_id_type=MESH)
-
-    def remote(src, dst, slot, device):
-        return pltpu.make_async_remote_copy(
-            src_ref=src,
-            dst_ref=dst,
-            send_sem=send_sem.at[slot],
-            recv_sem=recv_sem.at[slot],
-            device_id=device,
-            device_id_type=MESH,
-        )
-
-    spans = [(0, mid_lo), (mid_hi, slots), (mid_lo, mid_hi)]
-
-    def column(side, x, i, device):
-        lo, hi = spans[i]
-        span = pl.ds(lo, hi - lo)
-        return remote(comb.at[x, pl.ds(HALO + lo, hi - lo)], land.at[side, span], 3 * side + i, device)
-
-    to_east = [column(WEST, cols, i, east) for i in range(3)]
-    to_west = [column(EAST, 1, i, west) for i in range(3)]
-    up = remote(comb.at[pl.ds(1, cols), pl.ds(HALO, HALO)], bot_in, 6, above)
-    down = remote(tail, top_in, 7, below)
-
-    def up_side(side):
-        return remote(land.at[side, pl.ds(0, HALO)], bot_side.at[side], 8 + side, above)
-
-    def down_side(side):
-        return remote(tail_side.at[side], top_side.at[side], 10 + side, below)
-
-    @pl.when(has_above)
-    def _():
-        up.start()
-
-    @pl.when(has_below)
-    def _():
-        down.start()
-
-    @pl.when(jnp.logical_not(last))
     def _():
         for copy in to_east:
             copy.start()
-
-    @pl.when(jnp.logical_not(first))
-    def _():
-        for copy in to_west:
-            copy.start()
-
-    for load in loads[3:]:
-        load.wait()
-    pltpu.make_async_copy(uw, uw, local_sem.at[len(pairs)]).wait()
-    pltpu.make_async_copy(dw, dw, local_sem.at[len(pairs) + 1]).wait()
 
     for e in range(2):
         for row, ref in ((0, dg_ref), (1, db_ref)):
@@ -272,15 +332,7 @@
     ]
     step = PAIRS * sub
 
-    def compute(cells, ups, skip=0):
-        n = len(cells)
-        size = n * step
-        groups = sorted({(lo, hi) for lo, hi, _, _ in ups})
-
-        def coarse_at(i, e):
-            lo, hi = next(group for group in groups if group[0] <= i < group[1])
-            return 2 * lo * step + e * (hi - lo) * step + (i - lo) * step
-
+    def first_norm(cells, at=0):
         for i, (col, _, (spots, _, _)) in enumerate(cells):
             blocks = []
             for c in range(2):
@@ -298,12 +350,16 @@
                 for t, value in enumerate(values):
                     lane = slice(t * TILE, (t + 1) * TILE)
                     value = value * down_vec[2 * e : 2 * e + 1, lane] + down_vec[2 * e + 1 : 2 * e + 2, lane]
-                    nrm[e, i * step : (i + 1) * step, lane] = value.astype(BF16)
-        for e in range(2):
+                    nrm[e, pl.ds(pl.multiple_of((at + i) * step, step), step), lane] = value.astype(BF16)
+
+    def products(cells, ups, skip=0):
+        size = len(cells) * step
+        whole = len(ups) * size
+
+        def down(e):
             wide = jnp.dot(nrm[e, 0:size, :], dw[e], preferred_element_type=F32)
-            narrow = wide.astype(BF16)
+            coarse[e * size : (e + 1) * size, :] = wide.astype(BF16)
             for i, (_, merged_col, (_, _, merged_at)) in enumerate(cells):
-                coarse[coarse_at(i, e) : coarse_at(i, e) + step, :] = narrow[i * step : (i + 1) * step]
                 if merged_col is None or merged_at is None:
                     continue
                 for p in range(PAIRS):
@@ -312,21 +368,25 @@
                         turn_merged[
                             merged_at + skip, (2 * p + e) * 3 + t, pl.ds(merged_col, sub, stride=half_cols), :
                         ] = wide[at : at + sub, t * TILE : (t + 1) * TILE]
-        whole = sum(hi - lo for lo, hi, _, _ in ups) * step
-        off = 0
-        offs = []
-        for lo, hi, block, _ in ups:
-            part = (hi - lo) * step
-            spread = jnp.dot(coarse[2 * lo * step : 2 * hi * step, :], uw[block], preferred_element_type=F32)
-            for e in range(2):
-                for at in range(0, part, step):
-                    _, done = pair_norm([thirds(spread[e * part + at : e * part + at + step])], chan)
+
+        def widen(block, off, which):
+            rows = slice(which[0] * size, (which[-1] + 1) * size)
+            spread = jnp.dot(coarse[rows, :], uw[block], preferred_element_type=F32)
+            for e in which:
+                for at in range(0, size, step):
+                    lo = (e - which[0]) * size + at
+                    _, done = pair_norm([thirds(spread[lo : lo + step])], chan)
                     for t, value in enumerate(done[0]):
                         lane = slice(t * TILE, (t + 1) * TILE)
                         value = value * up_vec[0:1, lane] + up_vec[1:2, lane]
-                        renorm[e * whole + off + at : e * whole + off + at + step, lane] = value.astype(BF16)
-            offs.append(off)
-            off += part
+                        to = e * whole + off + at
+                        renorm[to : to + step, lane] = value.astype(BF16)
+
+        for which in PARITIES:
+            for e in which:
+                down(e)
+            for u, (block, _) in enumerate(ups):
+                widen(block, u * size, which)
         for a in range(2):
             two = [
                 jnp.dot(
@@ -336,11 +396,10 @@
                 )
                 for e in range(2)
             ]
-            for (lo, hi, _, x), off in zip(ups, offs):
-                for i in range(lo, hi):
-                    _, _, (_, fine_at, _) = cells[i]
+            for u, (_, x) in enumerate(ups):
+                for i, (_, _, (_, fine_at, _)) in enumerate(cells):
                     for p in range(PAIRS):
-                        at = off + (i - lo) * step + p * sub
+                        at = u * size + i * step + p * sub
                         span = slice(at, at + sub)
                         trio = (
                             two[0][span, 0:TILE],
@@ -350,15 +409,20 @@
                         for t, value in enumerate(trio):
                             turn_fine[fine_at + a, 3 * p + t, pl.ds(x, sub, stride=cols), :] = value
 
+    own_ups = [(0, 1), (1, 2)]
+
+    def compute_own(rows):
+        cells = [(2, 1, row) for row in rows]
+        first_norm(cells)
+        products(cells, own_ups)
+
     own = pl.ds(1, cols)
 
-    with jax.named_scope("c_own_inner"):
-        compute([(2, 1, row) for row in inner_rows], [(0, inner, 0, 1), (0, inner, 1, 2)])
-
-    @pl.when(last)
-    def _():
-        for copy in to_east:
-            copy.start()
+    with jax.named_scope("n_own"):
+        first_norm([(2, 1, row) for row in inner_rows])
+
+    with jax.named_scope("c_own"):
+        products([(2, 1, row) for row in inner_rows], own_ups)
 
     with jax.named_scope("w_halo"):
 
@@ -383,49 +447,40 @@
         def _():
             comb[:, 0:HALO] = jnp.zeros((cols + 2, HALO, sub, lanes), BF16)
 
+    def start_wrap():
+        for copy in to_west:
+            copy.start()
+
     with jax.named_scope("w_wrap"):
 
         @pl.when(first)
         def _():
-            pl.semaphore_wait(wrap_sem, 1)
-            for copy in to_west:
-                copy.start()
-
-    cross_lo = has_above & (lax.rem(lat, 2) == 0)
-    cross_hi = has_below & (lax.rem(lat, 2) == 1)
-    wrap_top_send = pltpu.make_async_remote_copy(
-        src_ref=top_in.at[cols - 1],
-        dst_ref=top_side.at[WEST],
-        send_sem=send_sem.at[12],
-        recv_sem=recv_sem.at[10 + WEST],
-        device_id=east,
-        device_id_type=MESH,
-    )
-    wrap_bot_send = pltpu.make_async_remote_copy(
-        src_ref=bot_in.at[cols - 1],
-        dst_ref=bot_side.at[WEST],
-        send_sem=send_sem.at[12],
-        recv_sem=recv_sem.at[8 + WEST],
-        device_id=east,
-        device_id_type=MESH,
-    )
-
-    @pl.when(last & cross_lo)
-    def _():
-        wrap_top_send.start()
-
-    @pl.when(last & cross_hi)
-    def _():
-        wrap_bot_send.start()
+            pl.semaphore_wait(ready_sem.at[2], 1)
+
+        @pl.when(first & (lat < n_lat // 2))
+        def _():
+            start_wrap()
+
+    for side, x, device in ((WEST, cols - 1, east), (EAST, 0, west)):
+
+        @pl.when(cross_lo & sends_cross(side))
+        def _():
+            cross(side, x, device, top_in, top_side, 10).start()
+
+        @pl.when(cross_hi & sends_cross(side))
+        def _():
+            cross(side, x, device, bot_in, bot_side, 8).start()
 
     outer = top_rows + bottom_rows
-    edges = len(outer)
     with jax.named_scope("c_own_outer"):
-        compute([(2, 1, row) for row in outer], [(0, edges, 0, 1), (0, edges, 1, 2)])
+        compute_own(outer)
 
     odd = lax.rem(lon, 2) == 1
     side_one = jnp.where(first | (odd & jnp.logical_not(last)), EAST, WEST)
     side_two = 1 - side_one
+
+    def spared(side):
+        return takes_cross(side) & cross_lo, takes_cross(side) & cross_hi
 
     def arrive(side):
         x = side * (cols + 1)
@@ -436,21 +491,22 @@
         for i in range(HALO):
             tail_side[side, i] = comb[x, count + i]
 
-        skip = first & (side == WEST)
-
-        @pl.when(has_above & jnp.logical_not(skip & cross_lo))
+        lo_spared, hi_spared = spared(side)
+
+        @pl.when(has_above & jnp.logical_not(lo_spared))
         def _():
             up_side(side).start()
 
-        @pl.when(has_below & jnp.logical_not(skip & cross_hi))
+        @pl.when(has_below & jnp.logical_not(hi_spared))
         def _():
             down_side(side).start()
 
+    def arrive_rest(side):
+        x = side * (cols + 1)
         lo, hi = spans[2]
         column(side, cols, 2, east).wait_recv()
         comb[x, HALO + lo : HALO + hi] = land[side, lo:hi]
 
-
     def corner(side):
         x = side * (cols + 1)
 
@@ -464,43 +520,113 @@
             up_side(side).wait_recv()
             comb[x, HALO + slots : total] = bot_side[side]
 
-    side_rows = top_rows + inner_rows + bottom_rows
-    for name, side in (("one", side_one), ("two", side_two)):
-        with jax.named_scope("w_" + name):
-            arrive(side)
-        with jax.named_scope("k_" + name):
-            corner(side)
-        with jax.named_scope("c_" + name):
-            compute(
-                [(side * cols, 0, row) for row in side_rows],
-                [(0, len(side_rows), 1 - side, side * (cols - 1))],
-                skip=side * (inner + BOTTOM + 1),
-            )
-
-    for copy in to_east + to_west:
-        copy.wait_send()
+    def ready(row):
+        _, fine_at, _ = row
+        return fine_at - 2 * TOP >= mid_hi
+
+    early = [row for row in inner_rows if ready(row)]
+    late = [row for row in inner_rows if not ready(row)]
+    side_rows = early + late + outer
+    assert len(late) == len(outer)
+
+    def place_of(rows):
+        return [row[1] for row in side_rows].index(rows[0][1])
+
+    def norm_side(side, rows):
+        first_norm([(side * cols, 0, row) for row in rows], place_of(rows))
+
+    def finish_side(side):
+        cells = [(side * cols, 0, row) for row in side_rows]
+        products(cells, [(1 - side, side * (cols - 1))], side * (inner + BOTTOM + 1))
+
+    hasty = first & (lax.rem(lat, 2) == 1)
+    with jax.named_scope("w_one"):
+        arrive(side_one)
+        arrive_rest(side_one)
+    with jax.named_scope("n_one"):
+        norm_side(side_one, early)
+        norm_side(side_one, late)
+    @pl.when(first & (lat >= n_lat // 2))
+    def _():
+        start_wrap()
+
+    with jax.named_scope("w_hasty"):
+
+        @pl.when(hasty)
+        def _():
+            arrive(side_two)
+
+    with jax.named_scope("k_one"):
+        corner(side_one)
+    with jax.named_scope("c_one"):
+        norm_side(side_one, outer)
+        finish_side(side_one)
+    with jax.named_scope("w_two"):
+
+        @pl.when(jnp.logical_not(hasty))
+        def _():
+            arrive(side_two)
+
+    with jax.named_scope("n_two"):
+        norm_side(side_two, early)
+
+    def chosen(own, other):
+        spots = [[jnp.where(hasty, x, y) for x, y in zip(a[0], b[0])] for a, b in zip(own, other)]
+        at = jnp.where(hasty, place_of(own), place_of(other))
+        first_norm([(side_two * cols, 0, (spot, None, None)) for spot in spots], at)
+
+    @pl.when(hasty)
+    def _():
+        arrive_rest(side_two)
+
+    @pl.when(jnp.logical_not(hasty))
+    def _():
+        with jax.named_scope("k_two"):
+            corner(side_two)
+
+    with jax.named_scope("m_two"):
+        chosen(late, outer)
+
+    @pl.when(hasty)
+    def _():
+        with jax.named_scope("kh_two"):
+            corner(side_two)
+
+    @pl.when(jnp.logical_not(hasty))
+    def _():
+        with jax.named_scope("r_two"):
+            arrive_rest(side_two)
+
+    with jax.named_scope("c_two"):
+        chosen(outer, late)
+        finish_side(side_two)
+
+    whole_column = comb.at[1, pl.ds(HALO, slots)]
+    for side, device in ((WEST, east), (EAST, west)):
+        remote(whole_column, land.at[side], side, device, 3 * side).wait_send()
 
     @pl.when(has_above)
     def _():
         up.wait_send()
-        up_side(EAST).wait_send()
 
     @pl.when(has_below)
     def _():
         down.wait_send()
-        down_side(EAST).wait_send()
-
-    @pl.when(has_above & jnp.logical_not(first & cross_lo))
-    def _():
-        up_side(WEST).wait_send()
-
-    @pl.when(has_below & jnp.logical_not(first & cross_hi))
-    def _():
-        down_side(WEST).wait_send()
-
-    @pl.when(last & (cross_lo | cross_hi))
-    def _():
-        wrap_top_send.wait_send()
+
+    for side, x, device in ((WEST, cols - 1, east), (EAST, 0, west)):
+        lo_spared, hi_spared = spared(side)
+
+        @pl.when(has_above & jnp.logical_not(lo_spared))
+        def _():
+            up_side(side).wait_send()
+
+        @pl.when(has_below & jnp.logical_not(hi_spared))
+        def _():
+            down_side(side).wait_send()
+
+        @pl.when((cross_lo | cross_hi) & sends_cross(side))
+        def _():
+            cross(side, x, device, top_in, top_side, 10).wait_send()
 
 
 def write_out(turn_merged, turn_fine, places, merged_hbm, fine_hbm, merged_buf, fine_buf, sem):
@@ -628,10 +754,10 @@
             pltpu.VMEM(down_bias.shape, F32),
             pltpu.VMEM(up_gain.shape, F32),
             pltpu.VMEM(up_bias.shape, F32),
+            pltpu.SemaphoreType.DMA((13,)),
             pltpu.SemaphoreType.DMA((10,)),
-            pltpu.SemaphoreType.DMA((13,)),
             pltpu.SemaphoreType.DMA((12,)),
-            pltpu.SemaphoreType.REGULAR,
+            pltpu.SemaphoreType.REGULAR((3,)),
         ],
         compiler_params=pltpu.CompilerParams(
             collective_id=0, has_side_effects=True, vmem_limit_bytes=48 * 2**20

time: 17.9 us -> 16.3 us (0.911)
  Pallas kernels: 17.1 us -> 15.5 us
    pallas_call x1, Pallas kernels: 16.1 us -> 14.4 us  [body(): pl.pallas_call(functools.partial(kernel, n_lat, n_lon), out_shape=(pltpu....]
where the time goes in v3:
time: 16.3 us; the launch traced here: 16.1 us
  Pallas kernels  15.5 us (95%)
  between operations  0.64 us (4%)
    pallas_call x1, Pallas kernels, body(): pl.pallas_call(functools.partial(kernel, n_lat, n_lon), out_shape=(pltpu....  14.4 us
    pallas_call x1, Pallas kernels, body(): pl.pallas_call(write_out, out_shape=(jax.ShapeDtypeStruct(merged_shape, B...  1.06 us

profile of v3, /device:TPU:0, one launch (start us, length us, event | category | flops | bytes accessed | tf_op | source)
XLA Modules:
  0.0 16.1 jit_solution(14947024034113416433)
XLA Ops:
  0.6 14.4 %shard_map.113 = (f32[19,12,16,128]{3,2,1,0:T(8,128)S(1)}, f32[23,6,32,128]{3,2,1,0:T(8,128)S(1)}, s32[4]{0:T(128)S(4)}) custom-call(s32[5]{0:T(128)} %in_b_hbm.1, s32[5]{0:T(128)} %out_b_hbm.1, bf16[4,14,4,1536]{3,2,1,0:T(4,128)(2,1)} %t_hbm.1, bf16[768,384]{1,0:T(8,128)(2,1)} %dw_hbm.1, bf16[384,768]{1,0:T(8,128)(2,1)} %uw_hbm.1, bf16[192,192]{1,0:T(8,128)(2,1)} %ow_hbm.1, ...), custom_call_target="tpu_custom_call" | custom-call | tf_op jit(solution)/shard_map/pallas_call | solution.py:722
  15.1 1.1 %shard_map.114 = (bf16[4,8,2,3072]{3,2,1,0:T(2,128)(2,1)}, bf16[4,14,4,1536]{3,2,1,0:T(4,128)(2,1)}) custom-call(f32[19,12,16,128]{3,2,1,0:T(8,128)S(1)} %get-tuple-element.5.turn_merged, f32[23,6,32,128]{3,2,1,0:T(8,128)S(1)} %get-tuple-element.6.turn_fine, s32[4]{0:T(128)S(4)} %get-tuple-element.7.places), custom_call_target="tpu_custom_call" | custom-call | tf_op jit(solution)/shard_map/pallas_call | solution.py:767

commit v4 on v3

--- a/solution.py
+++ b/solution.py
@@ -104,7 +104,8 @@
     tiles = lanes // TILE
     total = slots + 2 * HALO
     half_cols = cols // 2
-    inner = slots // 2
+    inner = slots // 2 - TOP
+    blank = inner + BOTTOM + TOP
     mid_lo, mid_hi = HALO, slots // 2
     lat = lax.axis_index("lat")
     lon = lax.axis_index("lon")
@@ -318,15 +319,21 @@
         ow_pad[1, a, a * short : a * short + chan, :] = moved
 
     turn_fine[2 * (TOP + inner + BOTTOM)] = jnp.zeros(turn_fine.shape[1:], F32)
-    turn_merged[inner + BOTTOM] = jnp.zeros(turn_merged.shape[1:], F32)
+    turn_merged[blank] = jnp.zeros(turn_merged.shape[1:], F32)
 
     def place(r):
         inside = jnp.maximum(r + shift - 1, 0)
         outside = jnp.minimum(HALO + slots + r - past, total - 1)
         return jnp.where(r < past, inside, outside)
 
-    top_rows = [([place(2 * m + a) for a in range(2)], 2 * m, None) for m in range(TOP)]
-    inner_rows = [([2 * m + a + shift - 1 for a in range(2)], 2 * m, m - TOP) for m in range(TOP, TOP + inner)]
+    def own_place(r):
+        return r + shift - 1
+
+    top_rows = []
+    for m, instead in ((0, shift < HALO), (1, shift == 0)):
+        spots = [jnp.where(instead, own_place(2 * (TOP + inner + m) + a), place(2 * m + a)) for a in range(2)]
+        top_rows.append((spots, 2 * m, inner + BOTTOM + m))
+    inner_rows = [([own_place(2 * m + a) for a in range(2)], 2 * m, m - TOP) for m in range(TOP, TOP + inner)]
     bottom_rows = [
         ([place(2 * (edge + i) + a) for a in range(2)], 2 * (TOP + inner + i), inner + i) for i in range(BOTTOM)
     ]
@@ -537,7 +544,7 @@
 
     def finish_side(side):
         cells = [(side * cols, 0, row) for row in side_rows]
-        products(cells, [(1 - side, side * (cols - 1))], side * (inner + BOTTOM + 1))
+        products(cells, [(1 - side, side * (cols - 1))], side * (blank + 1))
 
     hasty = first & (lax.rem(lat, 2) == 1)
     with jax.named_scope("w_one"):
@@ -635,7 +642,8 @@
     sub = turn_fine.shape[2] // cols
     halves = sub // members
     lanes = packed // halves
-    inner = slots // 2
+    inner = slots // 2 - TOP
+    blank = inner + BOTTOM + TOP
     count, shift, edge, count_out = places[0], places[1], places[2], places[3]
     copies = []
 
@@ -654,23 +662,25 @@
         copy.start()
         copies.append(copy)
 
-    for lo in range(0, merged_slots, 4):
-        hi = min(lo + 4, merged_slots)
-        for slot in range(lo, hi):
-            m = slot + TOP
-            index = jnp.where(m < edge, slot, jnp.minimum(inner + m - edge, inner + BOTTOM - 1))
-            index = jnp.where(slot < count_out, index, inner + BOTTOM)
-            put(turn_merged, index, slot, merged_buf, half_cols, 2 * lanes)
-        send(merged_buf, merged_hbm, lo, hi)
     for lo in range(0, slots, 5):
         hi = min(lo + 5, slots)
         for slot in range(lo, hi):
             r = slot + 2 * TOP - shift
             after = jnp.minimum(2 * (TOP + inner) + r - 2 * edge, 2 * (TOP + inner + BOTTOM) - 1)
-            index = jnp.where(r < 2 * edge, r, after)
+            before = jnp.where(r < 2 * (TOP + inner), r, r - 2 * (TOP + inner))
+            index = jnp.where(r < 2 * edge, before, after)
             index = jnp.where(slot < count, index, 2 * (TOP + inner + BOTTOM))
             put(turn_fine, index, slot, fine_buf, cols, lanes)
         send(fine_buf, fine_hbm, lo, hi)
+    for lo in range(0, merged_slots, 4):
+        hi = min(lo + 4, merged_slots)
+        for slot in range(lo, hi):
+            m = slot + TOP
+            index = min(slot if slot < inner else slot + BOTTOM, blank - 1)
+            index = jnp.where(m < edge, index, jnp.minimum(inner + m - edge, inner + BOTTOM - 1))
+            index = jnp.where(slot < count_out, index, blank)
+            put(turn_merged, index, slot, merged_buf, half_cols, 2 * lanes)
+        send(merged_buf, merged_hbm, lo, hi)
     for copy in copies:
         copy.wait()
 
@@ -694,7 +704,7 @@
     sub = halves * members
     merged_slots = slots // 2 + 1
     half_cols = cols // 2
-    inner = slots // 2
+    inner = slots // 2 - TOP
     edges = TOP + BOTTOM
     total = slots + 2 * HALO
     most = (inner + edges) * PAIRS * sub
@@ -722,7 +732,7 @@
     held = pl.pallas_call(
         functools.partial(kernel, n_lat, n_lon),
         out_shape=(
-            pltpu.VMEM((2 * (inner + BOTTOM) + 1, 2 * lanes // TILE, half_cols * sub, TILE), F32),
+            pltpu.VMEM((2 * (inner + edges + 1), 2 * lanes // TILE, half_cols * sub, TILE), F32),
             pltpu.VMEM((2 * (TOP + inner + BOTTOM) + 1, lanes // TILE, cols * sub, TILE), F32),
             pltpu.SMEM((4,), jnp.int32),
         ),

time: 16.3 us -> 16.2 us (level)
  no operation moved by 1% of the time
where the time goes in v4:
time: 16.2 us; the launch traced here: 16 us
  Pallas kernels  15.4 us (95%)
  between operations  0.64 us (4%)
    pallas_call x1, Pallas kernels, body(): pl.pallas_call(functools.partial(kernel, n_lat, n_lon), out_shape=(pltpu....  14.3 us
    pallas_call x1, Pallas kernels, body(): pl.pallas_call(write_out, out_shape=(jax.ShapeDtypeStruct(merged_shape, B...  1.06 us

profile of v4, /device:TPU:0, one launch (start us, length us, event | category | flops | bytes accessed | tf_op | source)
XLA Modules:
  0.0 16.0 jit_solution(10179190024237132446)
XLA Ops:
  0.6 14.3 %shard_map.113 = (f32[20,12,16,128]{3,2,1,0:T(8,128)S(1)}, f32[19,6,32,128]{3,2,1,0:T(8,128)S(1)}, s32[4]{0:T(128)S(4)}) custom-call(s32[5]{0:T(128)} %in_b_hbm.1, s32[5]{0:T(128)} %out_b_hbm.1, bf16[4,14,4,1536]{3,2,1,0:T(4,128)(2,1)} %t_hbm.1, bf16[768,384]{1,0:T(8,128)(2,1)} %dw_hbm.1, bf16[384,768]{1,0:T(8,128)(2,1)} %uw_hbm.1, bf16[192,192]{1,0:T(8,128)(2,1)} %ow_hbm.1, ...), custom_call_target="tpu_custom_call" | custom-call | tf_op jit(solution)/shard_map/pallas_call | solution.py:732
  15.0 1.1 %shard_map.114 = (bf16[4,8,2,3072]{3,2,1,0:T(2,128)(2,1)}, bf16[4,14,4,1536]{3,2,1,0:T(4,128)(2,1)}) custom-call(f32[20,12,16,128]{3,2,1,0:T(8,128)S(1)} %get-tuple-element.5.turn_merged, f32[19,6,32,128]{3,2,1,0:T(8,128)S(1)} %get-tuple-element.6.turn_fine, s32[4]{0:T(128)S(4)} %get-tuple-element.7.places), custom_call_target="tpu_custom_call" | custom-call | tf_op jit(solution)/shard_map/pallas_call | solution.py:777

commit v5 on v4

--- a/solution.py
+++ b/solution.py
@@ -149,16 +149,17 @@
         (ug_hbm, ug_ref),
         (ub_hbm, ub_ref),
     ]
-    loads = [pltpu.make_async_copy(src, dst, local_sem.at[3 + i]) for i, (src, dst) in enumerate(pairs)]
+    free_sems = [send_sem.at[i] for i in (3, 9, 4, 5, 6, 7, 8)]
+    loads = [pltpu.make_async_copy(src, dst, sem) for (src, dst), sem in zip(pairs, free_sems)]
     for load in loads:
         load.start()
     for block in range(2):
         cut = uw_hbm.at[:, pl.ds(block * 2 * chan, 2 * chan)]
-        pltpu.make_async_copy(cut, uw.at[block], local_sem.at[3 + len(pairs)]).start()
+        pltpu.make_async_copy(cut, uw.at[block], local_sem.at[3]).start()
     for pos, (e, start, size) in enumerate(down_pieces(chan)):
         at = sum(piece[2] for piece in down_pieces(chan)[:pos] if piece[0] == e)
         cut = dw_hbm.at[pl.ds(start, size)]
-        pltpu.make_async_copy(cut, dw.at[e, pl.ds(at, size)], local_sem.at[4 + len(pairs)]).start()
+        pltpu.make_async_copy(cut, dw.at[e, pl.ds(at, size)], local_sem.at[4]).start()
 
     def take_rows(lo, hi):
         for r in range(lo, hi):
@@ -295,8 +296,8 @@
 
     for load in loads[2:]:
         load.wait()
-    pltpu.make_async_copy(uw, uw, local_sem.at[3 + len(pairs)]).wait()
-    pltpu.make_async_copy(dw, dw, local_sem.at[4 + len(pairs)]).wait()
+    pltpu.make_async_copy(uw, uw, local_sem.at[3]).wait()
+    pltpu.make_async_copy(dw, dw, local_sem.at[4]).wait()
 
     @pl.when(last)
     def _():
@@ -764,7 +765,7 @@
             pltpu.VMEM(down_bias.shape, F32),
             pltpu.VMEM(up_gain.shape, F32),
             pltpu.VMEM(up_bias.shape, F32),
-            pltpu.SemaphoreType.DMA((13,)),
+            pltpu.SemaphoreType.DMA((5,)),
             pltpu.SemaphoreType.DMA((10,)),
             pltpu.SemaphoreType.DMA((12,)),
             pltpu.SemaphoreType.REGULAR((3,)),

time: 16.2 us -> 16.1 us (level)
  no operation moved by 1% of the time
where the time goes in v5:
time: 16.1 us; the launch traced here: 16 us
  Pallas kernels  15.3 us (95%)
  between operations  0.64 us (4%)
    pallas_call x1, Pallas kernels, body(): pl.pallas_call(functools.partial(kernel, n_lat, n_lon), out_shape=(pltpu....  14.3 us
    pallas_call x1, Pallas kernels, body(): pl.pallas_call(write_out, out_shape=(jax.ShapeDtypeStruct(merged_shape, B...  1.06 us

profile of v5, /device:TPU:0, one launch (start us, length us, event | category | flops | bytes accessed | tf_op | source)
XLA Modules:
  0.0 16.0 jit_solution(2369631810446610621)
XLA Ops:
  0.6 14.3 %shard_map.113 = (f32[20,12,16,128]{3,2,1,0:T(8,128)S(1)}, f32[19,6,32,128]{3,2,1,0:T(8,128)S(1)}, s32[4]{0:T(128)S(4)}) custom-call(s32[5]{0:T(128)} %in_b_hbm.1, s32[5]{0:T(128)} %out_b_hbm.1, bf16[4,14,4,1536]{3,2,1,0:T(4,128)(2,1)} %t_hbm.1, bf16[768,384]{1,0:T(8,128)(2,1)} %dw_hbm.1, bf16[384,768]{1,0:T(8,128)(2,1)} %uw_hbm.1, bf16[192,192]{1,0:T(8,128)(2,1)} %ow_hbm.1, ...), custom_call_target="tpu_custom_call" | custom-call | tf_op jit(solution)/shard_map/pallas_call | solution.py:733
  14.9 1.1 %shard_map.114 = (bf16[4,8,2,3072]{3,2,1,0:T(2,128)(2,1)}, bf16[4,14,4,1536]{3,2,1,0:T(4,128)(2,1)}) custom-call(f32[20,12,16,128]{3,2,1,0:T(8,128)S(1)} %get-tuple-element.5.turn_merged, f32[19,6,32,128]{3,2,1,0:T(8,128)S(1)} %get-tuple-element.6.turn_fine, s32[4]{0:T(128)S(4)} %get-tuple-element.7.places), custom_call_target="tpu_custom_call" | custom-call | tf_op jit(solution)/shard_map/pallas_call | solution.py:778

commit v6 on v5

--- a/solution.py
+++ b/solution.py
@@ -161,7 +161,7 @@
         cut = dw_hbm.at[pl.ds(start, size)]
         pltpu.make_async_copy(cut, dw.at[e, pl.ds(at, size)], local_sem.at[4]).start()
 
-    def take_rows(lo, hi):
+    def turn_rows(lo, hi):
         for r in range(lo, hi):
             for member in range(members):
                 row = t_ref[member, r].astype(F32)
@@ -170,7 +170,11 @@
                     for t in range(tiles):
                         lane = half * lanes + t * TILE
                         turn_in[r, t, at : at + cols, :] = row[:, lane : lane + TILE]
-        for x in range(cols):
+
+    sent, kept = (0, cols - 1), range(1, cols - 1)
+
+    def take_columns(lo, hi, columns):
+        for x in columns:
             for r in range(lo, hi):
                 for t in range(tiles):
                     comb[1 + x, HALO + r, :, t * TILE : (t + 1) * TILE] = turn_in[
@@ -197,7 +201,8 @@
 
     with jax.named_scope("w_tok"):
         token_loads[0].wait()
-    take_rows(*spans[0])
+    turn_rows(*spans[0])
+    take_columns(*spans[0], sent)
 
     def remote(src, dst, slot, device, landing=None):
         return pltpu.make_async_remote_copy(
@@ -254,17 +259,22 @@
             to_west[i].start()
 
     start_early(0)
+    take_columns(*spans[0], kept)
 
     @pl.when(has_above)
     def _():
         up.start()
 
     token_loads[1].wait()
-    take_rows(*spans[1])
+    turn_rows(*spans[1])
+    take_columns(*spans[1], sent)
     start_early(1)
+    take_columns(*spans[1], kept)
     token_loads[2].wait()
-    take_rows(*spans[2])
+    turn_rows(*spans[2])
+    take_columns(*spans[2], sent)
     start_early(2)
+    take_columns(*spans[2], kept)
 
     loads[0].wait()
     loads[1].wait()

time: 16.1 us -> 16.1 us (level)
  no operation moved by 1% of the time
where the time goes in v6:
time: 16.1 us; the launch traced here: 16 us
  Pallas kernels  15.3 us (95%)
  between operations  0.64 us (4%)
    pallas_call x1, Pallas kernels, body(): pl.pallas_call(functools.partial(kernel, n_lat, n_lon), out_shape=(pltpu....  14.3 us
    pallas_call x1, Pallas kernels, body(): pl.pallas_call(write_out, out_shape=(jax.ShapeDtypeStruct(merged_shape, B...  1.06 us

profile of v6, /device:TPU:0, one launch (start us, length us, event | category | flops | bytes accessed | tf_op | source)
XLA Modules:
  0.0 16.0 jit_solution(17619105069416430100)
XLA Ops:
  0.6 14.3 %shard_map.113 = (f32[20,12,16,128]{3,2,1,0:T(8,128)S(1)}, f32[19,6,32,128]{3,2,1,0:T(8,128)S(1)}, s32[4]{0:T(128)S(4)}) custom-call(s32[5]{0:T(128)} %in_b_hbm.1, s32[5]{0:T(128)} %out_b_hbm.1, bf16[4,14,4,1536]{3,2,1,0:T(4,128)(2,1)} %t_hbm.1, bf16[768,384]{1,0:T(8,128)(2,1)} %dw_hbm.1, bf16[384,768]{1,0:T(8,128)(2,1)} %uw_hbm.1, bf16[192,192]{1,0:T(8,128)(2,1)} %ow_hbm.1, ...), custom_call_target="tpu_custom_call" | custom-call | tf_op jit(solution)/shard_map/pallas_call | solution.py:743
  14.9 1.1 %shard_map.114 = (bf16[4,8,2,3072]{3,2,1,0:T(2,128)(2,1)}, bf16[4,14,4,1536]{3,2,1,0:T(4,128)(2,1)}) custom-call(f32[20,12,16,128]{3,2,1,0:T(8,128)S(1)} %get-tuple-element.5.turn_merged, f32[19,6,32,128]{3,2,1,0:T(8,128)S(1)} %get-tuple-element.6.turn_fine, s32[4]{0:T(128)S(4)} %get-tuple-element.7.places), custom_call_target="tpu_custom_call" | custom-call | tf_op jit(solution)/shard_map/pallas_call | solution.py:788
